TPU v7x, 128 devices: a whole 4x4x4 slice. The times are simulated.
128 devices in a mesh: layer: 32 (over x, z, y_hi), width: 4 (over y_lo, core).
Axes of the slice: x: 4, y: 4 (y_hi: 2, y_lo: 2; y = y_hi * 2 + y_lo), z: 4, core: 2. Of those that a mesh axis runs over, the one named last changes fastest.
Arguments:
- mlp_inputs: bfloat16 [32, 768, 4096], P('layer', None, 'width'), may hold values from -6 to 6
- mlp_outputs: bfloat16 [32, 768, 4096], P('layer', None, 'width'), may hold values from -6 to 6
- encoders: bfloat16 [32, 4096, 128], P('layer', 'width'), may hold values from -0.09375 to 0.09375
- encoder_bias: float32 [32, 128], P('layer'), may hold values from -0.5 to 0
- decoders: bfloat16 [32, 32, 128, 4096], P('layer', None, None, 'width'), may hold values from -0.1875 to 0.1875
Outputs:
- loss_mean: float32 [], replicated
- grad_encoders: bfloat16 [32, 4096, 128], P('layer', 'width')
- grad_encoder_bias: float32 [32, 128], P('layer')
- grad_decoders: bfloat16 [32, 32, 128, 4096], P('layer', None, None, 'width')
All inputs are finite; a program needn't handle non-finite values.
Results may differ from a plain program's by a relative error of at most 0.0055.
Values may be sent and summed in bfloat16 or wider, within the bound.
No kernel may reach another device: no remote copies, remote signals or barrier semaphores. Data moves between devices by JAX's collectives and lax.ppermute only.
A program may use at most 128 MiB of HBM per device.

v0:
```python
import functools
import itertools

import jax
import jax.numpy as jnp
from jax import lax
from jax.experimental import pallas as pl
from jax.experimental.pallas import tpu as pltpu
from jax.sharding import Mesh
from jax.sharding import PartitionSpec as P

AXES = ("x", "z", "yh", "yl", "c")
LAYER = ("x", "z", "yh")
WIDTH = ("yl", "c")
SWAP = [(0, 1), (1, 0)]
RING = 4
EXTRA = 16
INTERPRET = False

sparsity = 8.0
f32, bf16 = jnp.float32, jnp.bfloat16


def flat(x, z, y, c):
    return ((x % RING * RING + z % RING) * RING + y % RING) * 2 + c


def toward(shift, back=False):
    pairs = []
    for x, z, y, c in itertools.product(range(RING), range(RING), range(RING), range(2)):
        if c == 0:
            there = {1: (x + 1, z, y), 3: (x - 1, z, y), 2: (x, z, y + 1)}[shift]
        else:
            there = {1: (x, z + 1, y), 3: (x, z - 1, y), 2: (x, z, y - 1)}[shift]
        pair = (flat(x, z, y, c), flat(*there, c))
        pairs.append(pair[::-1] if back else pair)
    return pairs


COSETS = [
    [flat(x, f - x - 2 * yl, 2 * yh + yl, c) for x in range(RING) for yh in range(2) for yl in range(2)]
    for f in range(RING)
    for c in range(2)
]


def sent(array, shift, back=False):
    return lax.ppermute(array, AXES, toward(shift, back))


def in_coset(blocks):
    return lax.all_to_all(blocks, AXES, 0, 0, axis_index_groups=COSETS, tiled=True)


def swapped(array, axis):
    return lax.ppermute(array, axis, SWAP)


def halves(array, axis, dim=0):
    half = array.shape[dim] // 2
    own = lax.axis_index(axis)
    mine = lax.dynamic_slice_in_dim(array, own * half, half, dim)
    theirs = lax.dynamic_slice_in_dim(array, (1 - own) * half, half, dim)
    return mine, theirs


def pair_of(place, offset, turn, x):
    return RING * x + lax.rem(place[0] + offset + 2 * turn + RING - x, RING)


ORDER = tuple(itertools.product(range(2), range(RING)))
CHIP = pl.BlockSpec(memory_space=pltpu.VMEM)
SCALARS = pl.BlockSpec(memory_space=pltpu.SMEM)
FAR = pl.BlockSpec(memory_space=pltpu.HBM)


def near(array):
    return array if INTERPRET else pltpu.with_memory_space_constraint(array, pltpu.VMEM)


def far(array):
    return array if INTERPRET else pltpu.with_memory_space_constraint(array, pltpu.HBM)


def near_out(shape, kind):
    return jax.ShapeDtypeStruct(shape, kind) if INTERPRET else pltpu.VMEM(shape, kind)


def call(kernel, args, specs, outs, out_specs, scratch=(), flops=0, traffic=0, mib=16, **more):
    return pl.pallas_call(
        kernel,
        in_specs=specs,
        out_specs=out_specs,
        out_shape=outs,
        scratch_shapes=list(scratch),
        interpret=INTERPRET,
        compiler_params=pltpu.CompilerParams(vmem_limit_bytes=mib << 20),
        cost_estimate=pl.CostEstimate(flops=flops, bytes_accessed=traffic, transcendentals=0),
        **more,
    )(*args)


def load_kernel(source, out, sem):
    copy = pltpu.make_async_copy(source, out, sem)
    copy.start()
    copy.wait()


def loaded(array):
    return call(
        load_kernel,
        [far(array)],
        [FAR],
        near_out(array.shape, array.dtype),
        CHIP,
        [pltpu.SemaphoreType.DMA],
        flops=array.size * 400,
        traffic=array.size * 4,
        mib=1,
    )


def quarters(turn, quarter):
    first = slice(turn * quarter, (turn + 1) * quarter)
    second = slice((1 - turn) * quarter, (2 - turn) * quarter)
    return first, second


def lay_out(place, offset, sides, lhs):
    half = lhs.shape[0] // len(sides)
    latent = sides[0][0].shape[2]
    for i, (turn, x) in enumerate(ORDER):
        rows_a, rows_b = quarters(turn, half // 2)
        for yh in range(2):
            layer = 2 * pair_of(place, offset, turn, x) + yh
            at = 4 * x + 2 * yh
            lanes = slice((2 * i + yh) * latent, (2 * i + yh + 1) * latent)

            @pl.when(layer <= place[1])
            def _():
                for side, (a, b) in enumerate(sides):
                    block = lhs.at[side * half : (side + 1) * half]
                    block[rows_a, lanes] = a[at + turn]
                    block[rows_b, lanes] = b[at + 1 - turn]

            @pl.when(layer > place[1])
            def _():
                lhs[:, lanes] = jnp.zeros((lhs.shape[0], latent), lhs.dtype)


def forward_kernel(offset, last, tokens, place, a, b, w, v, *rest):
    half = 2 * a.shape[1]
    columns = w.shape[2]
    if last:
        before, outputs, other, signal, signal_other, squares, lhs, wanted, wanted_other, sems = rest
        rows = pl.ds(pl.multiple_of(place[2] * half, 16), half)
        copy = pltpu.make_async_copy(outputs.at[rows, :], wanted, sems.at[0])
        copy.start()
        copy_other = pltpu.make_async_copy(other, wanted_other, sems.at[1])
        copy_other.start()
    else:
        total, lhs = rest
    lay_out(place, offset, [(a, b)], lhs)
    step = min(512, columns)
    pairs = [pair_of(place, offset, turn, x) for turn, x in ORDER]
    carry = jnp.zeros((16, 128), f32)
    for side, source in enumerate((w, v)):
        if last and side == 0:
            target, out = wanted, signal
        elif last:
            target, out = wanted_other, signal_other
        for start in range(0, columns, step):
            cols = slice(start, start + step)
            both = slice(side * columns + start, side * columns + start + step)
            rhs = jnp.concatenate([source[pair, :, cols] for pair in pairs], axis=0)
            product = jnp.dot(lhs[...], rhs, preferred_element_type=f32)
            if not last:
                total[:, both] = product
                continue
            if side == 0 and start == 0:
                copy.wait()
                copy_other.wait()
            misfit = product + before[:, both] - target[:, cols].astype(f32)
            out[:, cols] = (misfit * (1.0 / tokens)).astype(bf16)
            square = misfit * misfit
            square = jnp.sum(square.reshape(-1, 16, step), axis=0)
            for lane in range(0, step, 128):
                carry = carry + square[:, lane : lane + 128]
    if last:
        squares[...] = carry


def forward(offset, place, a, b, w, v, extra=None, tokens=None):
    quarter, latent = a.shape[1:]
    half = 2 * quarter
    depth, columns = w.shape[1:]
    last = extra is not None
    args = [place] + [near(t) for t in (a, b, w, v)]
    specs = [SCALARS] + [CHIP] * 4
    scratch = [pltpu.VMEM((half, 16 * latent), bf16)]
    if last:
        before, outputs, wanted_other = extra
        args += [near(before), far(outputs), far(wanted_other)]
        specs += [CHIP, FAR, FAR]
        outs = (near_out((half, columns), bf16), near_out((half, columns), bf16), near_out((16, 128), f32))
        out_specs = (CHIP,) * 3
        scratch += [pltpu.VMEM((half, columns), bf16)] * 2 + [pltpu.SemaphoreType.DMA((2,))]
    else:
        outs, out_specs = near_out((half, 2 * columns), f32), CHIP
    flops = 2 * half * 2 * columns * 8 * depth
    kernel = functools.partial(forward_kernel, offset, last, tokens)
    return call(kernel, args, specs, outs, out_specs, scratch, flops, 1 << 20)


def terms_kernel(offset, place, signal, signal_other, w, v, squares, fired, a, b):
    quarter, latent = a.shape[1] - EXTRA, a.shape[2]
    contract = (((1,), (1,)), ((), ()))
    loss = 0.5 * jnp.sum(squares[...]) + sparsity * jnp.sum(fired[...])
    loss = jnp.full((8, latent), loss, f32)
    high = loss.astype(bf16).astype(f32)
    note = jnp.concatenate([high, loss - high], axis=0).astype(bf16)
    for tile in range(a.shape[0]):
        a[tile, quarter:, :] = note
        b[tile, quarter:, :] = note
    for turn in range(2):
        pairs = [pair_of(place, offset, turn, x) for x in range(RING)]
        rows_a, rows_b = quarters(turn, quarter)
        term = None
        for left, right in ((signal, w), (signal_other, v)):
            rhs = jnp.concatenate([right[pair] for pair in pairs], axis=0)
            part = lax.dot_general(left[...], rhs, contract, preferred_element_type=f32)
            term = part if term is None else term + part
        term = term.astype(bf16)
        for x, yh in itertools.product(range(RING), range(2)):
            at = 4 * x + 2 * yh
            lanes = slice((2 * x + yh) * latent, (2 * x + yh + 1) * latent)
            kept = jnp.where(2 * pairs[x] + yh <= place[1], term[:, lanes], jnp.zeros((), bf16))
            a[at + turn, :quarter, :] = kept[rows_a]
            b[at + 1 - turn, :quarter, :] = kept[rows_b]


def terms_for(offset, place, signal, signal_other, w, v, squares, fired):
    half, columns = signal.shape
    depth = w.shape[1]
    latent = depth // 2
    args = [place] + [near(t) for t in (signal, signal_other, w, v, squares, fired)]
    out = near_out((16, half // 2 + EXTRA, latent), bf16)
    flops = 2 * half * 2 * columns * 8 * depth
    kernel = functools.partial(terms_kernel, offset)
    return call(kernel, args, [SCALARS] + [CHIP] * 6, (out, out), (CHIP, CHIP), (), flops, 1 << 20)


def gradient_kernel(offset, place, a, b, a_other, b_other, signal, signal_other, *rest):
    out, lhs, rhs, held, sems = rest[-5:]
    half = signal.shape[0]
    depth = held.shape[1]
    rhs[:half, :] = signal[...]
    rhs[half:, :] = signal_other[...]
    lay_out(place, offset, [(a, b), (a_other, b_other)], lhs)
    contract = (((0,), (0,)), ((), ()))
    copies = []
    for i in range(0, len(ORDER), 2):
        left = lhs[:, i * depth : (i + 2) * depth]
        product = lax.dot_general(left, rhs[...], contract, preferred_element_type=f32).astype(bf16)
        for j in range(2):
            held[i + j] = product[j * depth : (j + 1) * depth]
            pair = pair_of(place, offset, *ORDER[i + j])
            copy = pltpu.make_async_copy(held.at[i + j], out.at[pair], sems.at[i + j])
            copy.start()
            copies.append(copy)
    for copy in copies:
        copy.wait()


def gradient(offset, place, a, b, a_other, b_other, signal, signal_other, so_far=None):
    latent = a.shape[2]
    half, columns = signal.shape
    args = [place] + [near(t) for t in (a, b, a_other, b_other)] + [signal, signal_other]
    specs = [SCALARS] + [CHIP] * 6
    aliases = {}
    if so_far is not None:
        aliases = {len(args): 0}
        args.append(so_far)
        specs.append(FAR)
    scratch = [
        pltpu.VMEM((2 * half, 16 * latent), bf16),
        pltpu.VMEM((2 * half, columns), bf16),
        pltpu.VMEM((len(ORDER), 2 * latent, columns), bf16),
        pltpu.SemaphoreType.DMA((len(ORDER),)),
    ]
    out = jax.ShapeDtypeStruct((RING * RING, 2 * latent, columns), bf16)
    flops = 2 * 2 * half * columns * 16 * latent
    kernel = functools.partial(gradient_kernel, offset)
    return call(kernel, args, specs, out, FAR, scratch, flops, 1 << 20, mib=20, input_output_aliases=aliases)


def sum_kernel(own, one, two, three, out):
    quarter = own.shape[1] - EXTRA
    parts = (own, one, two, three)
    for tile in range(own.shape[0]):
        total = functools.reduce(lambda s, p: s + p, [p[tile, :quarter, :].astype(f32) for p in parts])
        out[tile, :quarter, :] = total.astype(bf16)
        row = lax.broadcasted_iota(jnp.int32, (EXTRA, own.shape[2]), 0)
        note = jnp.zeros((EXTRA, own.shape[2]), f32)
        for i, part in enumerate(parts):
            heard = part[tile, quarter:, :].astype(f32)
            high = jnp.broadcast_to(heard[:1], heard.shape)
            low = jnp.broadcast_to(heard[8:9], heard.shape)
            note = jnp.where(row == 2 * i, high, jnp.where(row == 2 * i + 1, low, note))
        out[tile, quarter:, :] = note.astype(bf16)


def summed(*parts):
    args = [near(part) for part in parts]
    out = jax.ShapeDtypeStruct(parts[0].shape, bf16)
    return call(sum_kernel, args, [CHIP] * 4, out, CHIP, (), 1 << 20, 1 << 20, mib=4)


def delta_kernel(tokens, arrived, potential, delta, loss):
    quarter = potential.shape[0]
    total = arrived[0, :quarter, :].astype(f32)
    for tile in range(1, arrived.shape[0]):
        total = total + arrived[tile, :quarter, :].astype(f32)
    total = jnp.where(potential[...] > 0, total + sparsity / tokens, 0.0)
    delta[...] = total.astype(bf16)
    losses = []
    for tile in range(arrived.shape[0]):
        notes = arrived[tile, quarter:, :].astype(f32)
        losses += [notes[2 * i : 2 * i + 1] + notes[2 * i + 1 : 2 * i + 2] for i in range(RING)]
    unit = jnp.maximum(functools.reduce(jnp.maximum, losses), 1e-30)
    whole = functools.reduce(lambda p, q: p + q, [jnp.round(value / unit * 65536.0) for value in losses])
    loss[...] = jnp.broadcast_to(whole * (unit / 65536.0), loss.shape)


def delta_of(arrived, potential, tokens):
    quarter, latent = potential.shape
    args = [near(arrived), potential]
    outs = (near_out((quarter, latent), bf16), near_out((8, latent), f32))
    kernel = functools.partial(delta_kernel, tokens)
    return call(kernel, args, [CHIP] * 2, outs, (CHIP, CHIP), (), 1 << 20, 1 << 20, mib=8)


def finish_kernel(size, place, inputs, own, beside, opposite, last, loss, loss_other, encoder, bias, mean, delta):
    quarter = own.shape[0]
    core, side = place[2], place[3]
    parts = ((own, core, side), (beside, core, 1 - side), (opposite, 1 - core, side), (last, 1 - core, 1 - side))
    for part, c, y in parts:
        delta[pl.ds(pl.multiple_of((2 * c + y) * quarter, 16), quarter), :] = part[...]
    contract = (((0,), (0,)), ((), ()))
    product = lax.dot_general(inputs[...], delta[...], contract, preferred_element_type=f32)
    encoder[...] = product.astype(bf16)
    bias[...] = jnp.sum(delta[...].astype(f32), axis=0, keepdims=True)
    mean[0, 0] = (jnp.max(loss[...]) + jnp.max(loss_other[...])) / size


def finished(size, place, inputs, *parts):
    tokens, columns = inputs.shape
    latent = parts[0].shape[1]
    args = [place] + [near(t) for t in (inputs, *parts)]
    outs = (
        jax.ShapeDtypeStruct((columns, latent), bf16),
        jax.ShapeDtypeStruct((1, latent), f32),
        jax.ShapeDtypeStruct((1, 1), f32),
    )
    scratch = [pltpu.VMEM((tokens, latent), bf16)]
    kernel = functools.partial(finish_kernel, size)
    return call(kernel, args, [SCALARS] + [CHIP] * 7, outs, (CHIP, CHIP, SCALARS), scratch, 1 << 20, 1 << 20, mib=8)


def whole_step(mlp_inputs, mlp_outputs, encoders, encoder_bias, decoders):
    inputs = mlp_inputs[0]
    tokens = inputs.shape[0]
    width = inputs.shape[1] * lax.axis_size(WIDTH)
    layers = lax.axis_size(LAYER)
    latent = encoders.shape[2]
    own_layer = lax.axis_index(LAYER)
    core, side = lax.axis_index("c"), lax.axis_index("yl")
    coset = lax.rem(lax.axis_index("x") + lax.axis_index("z") + 2 * side, RING)
    place = jnp.stack([coset, own_layer, core, side]).astype(jnp.int32)

    partial = jnp.dot(inputs, encoders[0], preferred_element_type=f32)
    mine, theirs = halves(partial, "c")
    heard = swapped(theirs, "c")
    weights = decoders[0].reshape(layers // 2, 2 * latent, -1)
    outputs = mlp_outputs[0]
    heard, weights, outputs = lax.optimization_barrier((heard, weights, outputs))
    partial = mine + heard
    weights_other = swapped(weights, "c")
    mine, theirs = halves(partial, "yl")
    heard = swapped(theirs, "yl")
    potential = mine + heard + encoder_bias[0][None, :]
    active = jnp.maximum(potential, 0.0)
    firing = active.astype(bf16)
    fired = jnp.sum(active.reshape(-1, 8, latent), axis=0)

    own = in_coset(jnp.broadcast_to(firing[None], (16, *firing.shape)))
    two = sent(own, 2)
    one = sent(own, 1)
    three = sent(own, 3)
    own_other = swapped(own, "c")
    two_other = swapped(two, "c")
    one_other = swapped(one, "c")
    three_other = swapped(three, "c")
    own, outputs = lax.optimization_barrier((own, outputs))
    half = tokens // 2
    wanted_sent = lax.dynamic_slice_in_dim(outputs, (1 - core) * half, half, 0)
    wanted_other = swapped(wanted_sent, "c")

    weights = loaded(weights)
    weights_other = loaded(weights_other)
    total = forward(0, place, own, two, weights, weights_other)
    signal, signal_other, squares = forward(
        1, place, three, one, weights, weights_other, (total, outputs, wanted_other), tokens
    )
    signal_here = swapped(signal_other, "c")

    rest = (place, signal, signal_other, weights, weights_other, squares, fired)
    to_three, to_one = terms_for(1, *rest)
    from_one = sent(to_one, 1, back=True)
    from_three = sent(to_three, 3, back=True)
    at_home, to_two = terms_for(0, *rest)
    from_two = sent(to_two, 2, back=True)
    signals = (signal, signal_here)
    grad_decoder = gradient(0, place, own, two, own_other, two_other, *signals)
    arrived = in_coset(summed(at_home, from_one, from_two, from_three))
    grad_decoder = gradient(1, place, three, one, three_other, one_other, *signals, grad_decoder)

    delta, loss = delta_of(arrived, potential, tokens)
    opposite = swapped(delta, "c")
    beside = swapped(delta, "yl")
    loss_other = swapped(loss, "c")
    last = swapped(beside, "c")
    size = float(tokens * width * layers)
    grad_encoder, grad_bias, loss_mean = finished(
        size, place, inputs, delta, beside, opposite, last, loss, loss_other
    )
    return (loss_mean[0, 0], grad_encoder[None], grad_bias, grad_decoder.reshape(decoders.shape))


def solution(mesh):
    finer = Mesh(mesh.devices.reshape(4, 4, 2, 2, 2), AXES)
    placed = (
        P(LAYER, None, WIDTH),
        P(LAYER, None, WIDTH),
        P(LAYER, WIDTH, None),
        P(LAYER, None),
        P(LAYER, None, None, WIDTH),
    )
    return jax.shard_map(
        whole_step,
        mesh=finer,
        in_specs=placed,
        out_specs=(P(), P(LAYER, WIDTH, None), P(LAYER, None), P(LAYER, None, None, WIDTH)),
        check_vma=False,
    )
```

profile of v0, /device:TPU:1, one launch (start us, length us, event | category | flops | bytes accessed | tf_op | source)
XLA Modules:
  0.0 126.1 jit_solution(11194715861258291444)
XLA Ops:
  0.6 0.0 copy-start
  0.7 0.9 copy-done
  1.6 2.0 %fusion = f32[768,128]{1,0:T(8,128)S(1)} fusion(bf16[1,1024,128]{2,1,0:T(8,128)(2,1)S(1)} %copy-done, bf16[1,768,1024]{2,1,0:T(8,128)(2,1)} %param.5), kind=kOutput, calls=%fused_computation | convolution fusion | flops 201326592 | bytes 2228224 | tf_op jit(solution)/shard_map/dot_general | solution.py:381
  3.6 1.5 %collective-permute-start = (f32[384,128]{1,0:T(8,128)S(1)}, f32[384,128]{1,0:T(8,128)S(1)}, u32[]{:S(2)}, u32[]{:S(2)}) collective-permute-start(f32[384,128]{1,0:T(8,128)S(1)} %constant_dynamic-slice_fusion.2), channel_id=1, source_target_pairs={{0,1},{1,0},{2,3},{3,2},{4,5},{5,4},{6,7},{7,6},{8,9},{9,8},{10,11... | collective-permute-start | bytes 589832 | tf_op jit(solution)/shard_map/ppermute | solution.py:56
  5.1 1.1 collective-permute-done
  6.1 0.4 collective-permute-start.4
  6.5 1.5 %collective-permute-start.1 = (f32[192,128]{1,0:T(8,128)S(1)}, f32[192,128]{1,0:T(8,128)S(1)}, u32[]{:S(2)}, u32[]{:S(2)}) collective-permute-start(f32[192,128]{1,0:T(8,128)S(1)} %constant_dynamic-slice_fusion.1), channel_id=1, source_target_pairs={{0,2},{2,0},{1,3},{3,1},{4,6},{6,4},{5,7},{7,5},{8,10},{10,8},{9,1... | collective-permute-start | bytes 294920 | tf_op jit(solution)/shard_map/ppermute | solution.py:56
  8.0 2.8 %collective-permute-done.1 = f32[192,128]{1,0:T(8,128)S(1)} collective-permute-done((f32[192,128]{1,0:T(8,128)S(1)}, f32[192,128]{1,0:T(8,128)S(1)}, u32[]{:S(2)}, u32[]{:S(2)}) %collective-permute-start.1) | collective-permute-done | bytes 98336 | tf_op jit(solution)/shard_map/ppermute | solution.py:56
  10.8 0.0 copy-done.8
  10.9 0.1 broadcast_in_dim.4
  11.0 24.2 %all_to_all.10.a = bf16[16,192,128]{2,1,0:T(8,128)(2,1)S(1)} all-to-all(bf16[16,192,128]{2,1,0:T(8,128)(2,1)S(1)} %broadcast_in_dim.4), channel_id=1, replica_groups={{0,18,4,22,56,42,60,46,80,66,84,70,104,122,108,126},{1,19,5,23,57,43,61..., dimensions={0} | all-to-all | bytes 1572864 | tf_op jit(solution)/shard_map/all_to_all | solution.py:52
  35.3 0.0 collective-permute-start.5
  35.3 2.1 %constant_dynamic-slice_fusion = bf16[384,1024]{1,0:T(8,128)(2,1)} fusion(bf16[768,1024]{1,0:T(8,128)(2,1)} %bitcast.22, s32[]{:T(128)S(6)} %select_n.14), kind=kLoop, calls=%fused_computation.6 | loop fusion | bytes 1572868 | tf_op jit(solution)/shard_map/dynamic_slice | solution.py:406
  37.3 2.0 %collective-permute-start.2 = (bf16[16,192,128]{2,1,0:T(8,128)(2,1)S(1)}, bf16[16,192,128]{2,1,0:T(8,128)(2,1)S(1)}, u32[]{:S(2)}, u32[]{:S(2)}) collective-permute-start(bf16[16,192,128]{2,1,0:T(8,128)(2,1)S(1)} %all_to_all.10.a), channel_id=1, source_target_pairs={{0,96},{1,25},{2,98},{3,27},{4,100},{5,29},{6,102},{7,31},{8,104},... | collective-permute-start | bytes 2359304 | tf_op jit(solution)/shard_map/ppermute | solution.py:48
  39.3 0.0 collective-permute-start.3
  39.3 2.7 %collective-permute-start.6 = (bf16[384,1024]{1,0:T(8,128)(2,1)}, bf16[384,1024]{1,0:T(8,128)(2,1)}, u32[]{:S(2)}, u32[]{:S(2)}) collective-permute-start(bf16[384,1024]{1,0:T(8,128)(2,1)} %constant_dynamic-slice_fusion), channel_id=1, source_target_pairs={{0,1},{1,0},{2,3},{3,2},{4,5},{5,4},{6,7},{7,6},{8,9},{9,8},{10,11... | collective-permute-start | bytes 2359304 | tf_op jit(solution)/shard_map/ppermute | solution.py:56
  42.0 0.1 pad_add_fusion.place
  42.1 3.4 %shard_map.84.w = bf16[16,256,1024]{2,1,0:T(8,128)(2,1)S(1)} custom-call(bf16[16,256,1024]{2,1,0:T(8,128)(2,1)} %bitcast.21), custom_call_target="tpu_custom_call" | custom-call | flops 1677721600 | bytes 16777216 | tf_op jit(solution)/shard_map/pallas_call | solution.py:90
  45.5 0.0 collective-permute-done.4.source
  45.5 3.4 %shard_map.85.v = bf16[16,256,1024]{2,1,0:T(8,128)(2,1)S(1)} custom-call(bf16[16,256,1024]{2,1,0:T(8,128)(2,1)} %collective-permute-done.4.source), custom_call_target="tpu_custom_call" | custom-call | flops 1677721600 | bytes 16777216 | tf_op jit(solution)/shard_map/pallas_call | solution.py:90
  48.9 0.0 collective-permute-done.5.b
  48.9 0.0 copy-start.6
  48.9 4.4 %shard_map.86.rest_0_ = f32[384,2048]{1,0:T(8,128)S(1)} custom-call(s32[4]{0:T(128)S(1)} %pad_add_fusion.place, bf16[16,192,128]{2,1,0:T(8,128)(2,1)S(1)} %all_to_all.10.a, bf16[16,192,128]{2,1,0:T(8,128)(2,1)S(1)} %collective-permute-done.5.b, bf16[16,256,1024]{2,1,0:T(8,128)(2,1)S(1)} %shard_map.84.w, bf16[16,256,1024]{2,1,0:T(8,128)(2,1)S(1)} %shard_map.85.v), custom_call_target="tpu_custom_call" | custom-call | flops 3221225472 | bytes 1048576 | tf_op jit(solution)/shard_map/pallas_call | solution.py:90
  53.4 0.0 collective-permute-done.2.a
  53.4 0.0 collective-permute-done.3.b
  53.4 0.0 collective-permute-done.6.rest_2_
  53.4 5.8 %shard_map.87 = (bf16[384,1024]{1,0:T(8,128)(2,1)S(1)}, bf16[384,1024]{1,0:T(8,128)(2,1)S(1)}, f32[16,128]{1,0:T(8,128)S(1)}) custom-call(s32[4]{0:T(128)S(1)} %pad_add_fusion.place, bf16[16,192,128]{2,1,0:T(8,128)(2,1)S(1)} %collective-permute-done.2.a, bf16[16,192,128]{2,1,0:T(8,128)(2,1)S(1)} %collective-permute-done.3.b, ...), custom_call_target="tpu_custom_call" | custom-call | flops 3221225472 | bytes 1048576 | tf_op jit(solution)/shard_map/pallas_call | solution.py:90
  59.2 4.1 %shard_map.88 = (bf16[16,208,128]{2,1,0:T(8,128)(2,1)S(1)}, bf16[16,208,128]{2,1,0:T(8,128)(2,1)S(1)}) custom-call(s32[4]{0:T(128)S(1)} %pad_add_fusion.place, bf16[384,1024]{1,0:T(8,128)(2,1)S(1)} %get-tuple-element.26.signal, bf16[384,1024]{1,0:T(8,128)(2,1)S(1)} %get-tuple-element.27.signal_other, bf16[16,256,1024]{2,1,0:T(8,128)(2,1)S(1)} %shard_map.84.w, ...), custom_call_target="tpu_custom_call" | custom-call | flops 3221225472 | bytes 1048576 | tf_op jit(solution)/shard_map/pallas_call | solution.py:90
  63.3 0.0 copy-done.5
  63.3 4.1 %shard_map.89 = (bf16[16,208,128]{2,1,0:T(8,128)(2,1)S(1)}, bf16[16,208,128]{2,1,0:T(8,128)(2,1)S(1)}) custom-call(s32[4]{0:T(128)S(1)} %pad_add_fusion.place, bf16[384,1024]{1,0:T(8,128)(2,1)S(1)} %get-tuple-element.26.signal, bf16[384,1024]{1,0:T(8,128)(2,1)S(1)} %get-tuple-element.27.signal_other, bf16[16,256,1024]{2,1,0:T(8,128)(2,1)S(1)} %shard_map.84.w, ...), custom_call_target="tpu_custom_call" | custom-call | flops 3221225472 | bytes 1048576 | tf_op jit(solution)/shard_map/pallas_call | solution.py:90
  67.3 1.8 %collective-permute-start.7 = (bf16[16,208,128]{2,1,0:T(8,128)(2,1)S(1)}, bf16[16,208,128]{2,1,0:T(8,128)(2,1)S(1)}, u32[]{:S(2)}, u32[]{:S(2)}) collective-permute-start(bf16[16,208,128]{2,1,0:T(8,128)(2,1)S(1)} %get-tuple-element.30), channel_id=1, source_target_pairs={{32,0},{9,1},{34,2},{11,3},{36,4},{13,5},{38,6},{15,7},{40,8},{17,... | collective-permute-start | bytes 2555912 | tf_op jit(solution)/shard_map/ppermute | solution.py:48
  69.2 0.0 collective-permute-start.8
  69.2 0.5 collective-permute-start.9
  69.6 9.6 %collective-permute-done.7.one = bf16[16,208,128]{2,1,0:T(8,128)(2,1)S(1)} collective-permute-done((bf16[16,208,128]{2,1,0:T(8,128)(2,1)S(1)}, bf16[16,208,128]{2,1,0:T(8,128)(2,1)S(1)}, u32[]{:S(2)}, u32[]{:S(2)}) %collective-permute-start.7) | collective-permute-done | bytes 852000 | tf_op jit(solution)/shard_map/ppermute | solution.py:48
  79.2 3.0 %collective-permute-done.8.two = bf16[16,208,128]{2,1,0:T(8,128)(2,1)S(1)} collective-permute-done((bf16[16,208,128]{2,1,0:T(8,128)(2,1)S(1)}, bf16[16,208,128]{2,1,0:T(8,128)(2,1)S(1)}, u32[]{:S(2)}, u32[]{:S(2)}) %collective-permute-start.8) | collective-permute-done | bytes 852000 | tf_op jit(solution)/shard_map/ppermute | solution.py:48
  82.2 0.0 collective-permute-done.9.three
  82.2 1.3 %shard_map.90 = bf16[16,208,128]{2,1,0:T(8,128)(2,1)} custom-call(bf16[16,208,128]{2,1,0:T(8,128)(2,1)S(1)} %get-tuple-element.29.own, bf16[16,208,128]{2,1,0:T(8,128)(2,1)S(1)} %collective-permute-done.7.one, bf16[16,208,128]{2,1,0:T(8,128)(2,1)S(1)} %collective-permute-done.8.two, bf16[16,208,128]{2,1,0:T(8,128)(2,1)S(1)} %collective-permute-done.9.three), custom_call_target="tpu_custom_call" | custom-call | flops 1048576 | bytes 1048576 | tf_op jit(solution)/shard_map/pallas_call | solution.py:90
  83.6 5.5 %all-to-all-start.1 = ((bf16[16,208,128]{2,1,0:T(8,128)(2,1)}), bf16[16,208,128]{2,1,0:T(8,128)(2,1)S(1)}, u32[]{:S(2)}, u32[]{:S(2)}) async-start(bf16[16,208,128]{2,1,0:T(8,128)(2,1)} %shard_map.90), calls=%async_computation.1 | async-start | bytes 1703936 | tf_op jit(solution)/shard_map/all_to_all | solution.py:52
  89.0 2.2 %collective-permute-start.17 = (bf16[16,192,128]{2,1,0:T(8,128)(2,1)S(1)}, bf16[16,192,128]{2,1,0:T(8,128)(2,1)}, u32[]{:S(2)}, u32[]{:S(2)}) collective-permute-start(bf16[16,192,128]{2,1,0:T(8,128)(2,1)S(1)} %all_to_all.10.a), channel_id=1, source_target_pairs={{0,1},{1,0},{2,3},{3,2},{4,5},{5,4},{6,7},{7,6},{8,9},{9,8},{10,11... | collective-permute-start | bytes 2359304 | tf_op jit(solution)/shard_map/ppermute | solution.py:56
  91.3 0.1 collective-permute-start.18
  91.4 0.4 collective-permute-start.16
  91.8 0.1 collective-permute-start.14
  91.9 0.4 collective-permute-start.15
  92.3 8.6 %all-to-all-done.1.arrived = bf16[16,208,128]{2,1,0:T(8,128)(2,1)S(1)} async-done(((bf16[16,208,128]{2,1,0:T(8,128)(2,1)}), bf16[16,208,128]{2,1,0:T(8,128)(2,1)S(1)}, u32[]{:S(2)}, u32[]{:S(2)}) %all-to-all-start.1) | async-done | bytes 852000 | tf_op jit(solution)/shard_map/all_to_all | solution.py:52
  100.9 0.2 shard_map.91
  101.2 0.0 collective-permute-done.17.a_other
  101.2 0.0 copy-start.4
  101.2 2.9 %collective-permute-start.10 = (bf16[192,128]{1,0:T(8,128)(2,1)S(1)}, bf16[192,128]{1,0:T(8,128)(2,1)S(1)}, u32[]{:S(2)}, u32[]{:S(2)}) collective-permute-start(bf16[192,128]{1,0:T(8,128)(2,1)S(1)} %get-tuple-element.33.own), channel_id=1, source_target_pairs={{0,2},{2,0},{1,3},{3,1},{4,6},{6,4},{5,7},{7,5},{8,10},{10,8},{9,1... | collective-permute-start | bytes 147464 | tf_op jit(solution)/shard_map/ppermute | solution.py:56
  104.1 0.0 collective-permute-done.18.b_other
  104.1 0.0 collective-permute-done.16.signal_other
  104.1 1.1 copy-done.7
  105.2 7.1 %shard_map.93.rest_0_ = bf16[16,256,1024]{2,1,0:T(8,128)(2,1)} custom-call(s32[4]{0:T(128)S(1)} %pad_add_fusion.place, bf16[16,192,128]{2,1,0:T(8,128)(2,1)S(1)} %all_to_all.10.a, bf16[16,192,128]{2,1,0:T(8,128)(2,1)S(1)} %copy-done.7, bf16[16,192,128]{2,1,0:T(8,128)(2,1)} %collective-permute-done.17.a_other, ...), custom_call_target="tpu_custom_call" | custom-call | flops 3221225472 | bytes 1048576 | tf_op jit(solution)/shard_map/pallas_call | solution.py:90
  112.3 3.9 %collective-permute-start.11 = (bf16[192,128]{1,0:T(8,128)(2,1)S(1)}, bf16[192,128]{1,0:T(8,128)(2,1)S(1)}, u32[]{:S(2)}, u32[]{:S(2)}) collective-permute-start(bf16[192,128]{1,0:T(8,128)(2,1)S(1)} %get-tuple-element.33.own), channel_id=1, source_target_pairs={{0,1},{1,0},{2,3},{3,2},{4,5},{5,4},{6,7},{7,6},{8,9},{9,8},{10,11... | collective-permute-start | bytes 147464 | tf_op jit(solution)/shard_map/ppermute | solution.py:56
  116.3 0.1 collective-permute-start.13
  116.4 0.0 collective-permute-done.10.beside
  116.4 0.4 collective-permute-start.12
  116.8 0.0 collective-permute-done.14.a_other
  116.8 0.0 collective-permute-done.15.b_other
  116.8 0.0 copy-start.1
  116.8 7.1 %shard_map.94 = bf16[16,256,1024]{2,1,0:T(8,128)(2,1)} custom-call(s32[4]{0:T(128)S(1)} %pad_add_fusion.place, bf16[16,192,128]{2,1,0:T(8,128)(2,1)S(1)} %collective-permute-done.2.a, bf16[16,192,128]{2,1,0:T(8,128)(2,1)S(1)} %copy-done.4, bf16[16,192,128]{2,1,0:T(8,128)(2,1)} %collective-permute-done.14.a_other, ...), custom_call_target="tpu_custom_call", output_to_operand_aliasing={{}: (7, {})} | custom-call | flops 3221225472 | bytes 1048576 | tf_op jit(solution)/shard_map/pallas_call | solution.py:90
  123.9 0.0 collective-permute-done.13.loss_other
  123.9 0.0 collective-permute-done.11.opposite
  123.9 0.0 collective-permute-done.12.last
  123.9 1.9 %shard_map.92 = (bf16[1024,128]{1,0:T(8,128)(2,1)}, f32[1,128]{1,0:T(1,128)}, f32[1,1]{1,0:T(1,128)}) custom-call(s32[4]{0:T(128)S(1)} %pad_add_fusion.place, bf16[768,1024]{1,0:T(8,128)(2,1)S(1)} %bitcast.18, bf16[192,128]{1,0:T(8,128)(2,1)S(1)} %get-tuple-element.33.own, bf16[192,128]{1,0:T(8,128)(2,1)S(1)} %collective-permute-done.10.beside, ...), custom_call_target="tpu_custom_call" | custom-call | flops 1048576 | bytes 1048576 | tf_op jit(solution)/shard_map/pallas_call | solution.py:90
  (15 shorter events, 0.1 us)
Async XLA Ops:
  0.6 1.0 copy-start
  0.6 10.2 %copy-start.8 = (f32[1,128]{1,0:T(1,128)S(1)}, f32[1,128]{1,0:T(1,128)}, u32[]{:S(2)}) copy-start(f32[1,128]{1,0:T(1,128)} %param.8) | copy-start | bytes 1540
  3.6 2.5 %collective-permute-start = (f32[384,128]{1,0:T(8,128)S(1)}, f32[384,128]{1,0:T(8,128)S(1)}, u32[]{:S(2)}, u32[]{:S(2)}) collective-permute-start(f32[384,128]{1,0:T(8,128)S(1)} %constant_dynamic-slice_fusion.2), channel_id=1, source_target_pairs={{0,1},{1,0},{2,3},{3,2},{4,5},{5,4},{6,7},{7,6},{8,9},{9,8},{10,11... | collective-permute-start | bytes 589832 | tf_op jit(solution)/shard_map/ppermute | solution.py:56
  6.1 39.4 %collective-permute-start.4 = (bf16[16,256,1024]{2,1,0:T(8,128)(2,1)}, bf16[16,256,1024]{2,1,0:T(8,128)(2,1)}, u32[]{:S(2)}, u32[]{:S(2)}) collective-permute-start(bf16[16,256,1024]{2,1,0:T(8,128)(2,1)} %bitcast.20), channel_id=1, source_target_pairs={{0,1},{1,0},{2,3},{3,2},{4,5},{5,4},{6,7},{7,6},{8,9},{9,8},{10,11... | collective-permute-start | bytes 25165832 | tf_op jit(solution)/shard_map/ppermute | solution.py:56
  6.5 4.3 %collective-permute-start.1 = (f32[192,128]{1,0:T(8,128)S(1)}, f32[192,128]{1,0:T(8,128)S(1)}, u32[]{:S(2)}, u32[]{:S(2)}) collective-permute-start(f32[192,128]{1,0:T(8,128)S(1)} %constant_dynamic-slice_fusion.1), channel_id=1, source_target_pairs={{0,2},{2,0},{1,3},{3,1},{4,6},{6,4},{5,7},{7,5},{8,10},{10,8},{9,1... | collective-permute-start | bytes 294920 | tf_op jit(solution)/shard_map/ppermute | solution.py:56
  35.3 13.6 %collective-permute-start.5 = (bf16[16,192,128]{2,1,0:T(8,128)(2,1)S(1)}, bf16[16,192,128]{2,1,0:T(8,128)(2,1)S(1)}, u32[]{:S(2)}, u32[]{:S(2)}) collective-permute-start(bf16[16,192,128]{2,1,0:T(8,128)(2,1)S(1)} %all_to_all.10.a), channel_id=1, source_target_pairs={{0,2},{1,7},{2,4},{3,1},{4,6},{5,3},{6,0},{7,5},{8,10},{9,15},{10,... | collective-permute-start | bytes 2359304 | tf_op jit(solution)/shard_map/ppermute | solution.py:48
  37.3 16.0 %collective-permute-start.2 = (bf16[16,192,128]{2,1,0:T(8,128)(2,1)S(1)}, bf16[16,192,128]{2,1,0:T(8,128)(2,1)S(1)}, u32[]{:S(2)}, u32[]{:S(2)}) collective-permute-start(bf16[16,192,128]{2,1,0:T(8,128)(2,1)S(1)} %all_to_all.10.a), channel_id=1, source_target_pairs={{0,96},{1,25},{2,98},{3,27},{4,100},{5,29},{6,102},{7,31},{8,104},... | collective-permute-start | bytes 2359304 | tf_op jit(solution)/shard_map/ppermute | solution.py:48
  39.3 14.0 %collective-permute-start.3 = (bf16[16,192,128]{2,1,0:T(8,128)(2,1)S(1)}, bf16[16,192,128]{2,1,0:T(8,128)(2,1)S(1)}, u32[]{:S(2)}, u32[]{:S(2)}) collective-permute-start(bf16[16,192,128]{2,1,0:T(8,128)(2,1)S(1)} %all_to_all.10.a), channel_id=1, source_target_pairs={{0,32},{1,9},{2,34},{3,11},{4,36},{5,13},{6,38},{7,15},{8,40},{9,1... | collective-permute-start | bytes 2359304 | tf_op jit(solution)/shard_map/ppermute | solution.py:48
  39.3 14.1 %collective-permute-start.6 = (bf16[384,1024]{1,0:T(8,128)(2,1)}, bf16[384,1024]{1,0:T(8,128)(2,1)}, u32[]{:S(2)}, u32[]{:S(2)}) collective-permute-start(bf16[384,1024]{1,0:T(8,128)(2,1)} %constant_dynamic-slice_fusion), channel_id=1, source_target_pairs={{0,1},{1,0},{2,3},{3,2},{4,5},{5,4},{6,7},{7,6},{8,9},{9,8},{10,11... | collective-permute-start | bytes 2359304 | tf_op jit(solution)/shard_map/ppermute | solution.py:56
  48.9 4.4 %copy-start.6 = (bf16[16,192,128]{2,1,0:T(8,128)(2,1)}, bf16[16,192,128]{2,1,0:T(8,128)(2,1)S(1)}, u32[]{:S(2)}) copy-start(bf16[16,192,128]{2,1,0:T(8,128)(2,1)S(1)} %collective-permute-done.5.b) | copy-start | bytes 2359300
  53.4 5.8 %copy-start.3 = (bf16[16,192,128]{2,1,0:T(8,128)(2,1)}, bf16[16,192,128]{2,1,0:T(8,128)(2,1)S(1)}, u32[]{:S(2)}) copy-start(bf16[16,192,128]{2,1,0:T(8,128)(2,1)S(1)} %collective-permute-done.3.b) | copy-start | bytes 2359300
  59.2 4.1 %copy-start.5 = (bf16[384,1024]{1,0:T(8,128)(2,1)}, bf16[384,1024]{1,0:T(8,128)(2,1)S(1)}, u32[]{:S(2)}) copy-start(bf16[384,1024]{1,0:T(8,128)(2,1)S(1)} %get-tuple-element.27.signal_other) | copy-start | bytes 2359300
  67.3 11.9 %collective-permute-start.7 = (bf16[16,208,128]{2,1,0:T(8,128)(2,1)S(1)}, bf16[16,208,128]{2,1,0:T(8,128)(2,1)S(1)}, u32[]{:S(2)}, u32[]{:S(2)}) collective-permute-start(bf16[16,208,128]{2,1,0:T(8,128)(2,1)S(1)} %get-tuple-element.30), channel_id=1, source_target_pairs={{32,0},{9,1},{34,2},{11,3},{36,4},{13,5},{38,6},{15,7},{40,8},{17,... | collective-permute-start | bytes 2555912 | tf_op jit(solution)/shard_map/ppermute | solution.py:48
  69.2 13.0 %collective-permute-start.8 = (bf16[16,208,128]{2,1,0:T(8,128)(2,1)S(1)}, bf16[16,208,128]{2,1,0:T(8,128)(2,1)S(1)}, u32[]{:S(2)}, u32[]{:S(2)}) collective-permute-start(bf16[16,208,128]{2,1,0:T(8,128)(2,1)S(1)} %get-tuple-element.31), channel_id=1, source_target_pairs={{2,0},{7,1},{4,2},{1,3},{6,4},{3,5},{0,6},{5,7},{10,8},{15,9},{12,... | collective-permute-start | bytes 2555912 | tf_op jit(solution)/shard_map/ppermute | solution.py:48
  69.2 13.0 %collective-permute-start.9 = (bf16[16,208,128]{2,1,0:T(8,128)(2,1)S(1)}, bf16[16,208,128]{2,1,0:T(8,128)(2,1)S(1)}, u32[]{:S(2)}, u32[]{:S(2)}) collective-permute-start(bf16[16,208,128]{2,1,0:T(8,128)(2,1)S(1)} %get-tuple-element.32), channel_id=1, source_target_pairs={{96,0},{25,1},{98,2},{27,3},{100,4},{29,5},{102,6},{31,7},{104,8},... | collective-permute-start | bytes 2555912 | tf_op jit(solution)/shard_map/ppermute | solution.py:48
  83.6 17.3 %all-to-all-start.1 = ((bf16[16,208,128]{2,1,0:T(8,128)(2,1)}), bf16[16,208,128]{2,1,0:T(8,128)(2,1)S(1)}, u32[]{:S(2)}, u32[]{:S(2)}) async-start(bf16[16,208,128]{2,1,0:T(8,128)(2,1)} %shard_map.90), calls=%async_computation.1 | async-start | bytes 1703936 | tf_op jit(solution)/shard_map/all_to_all | solution.py:52
  89.0 12.1 %collective-permute-start.17 = (bf16[16,192,128]{2,1,0:T(8,128)(2,1)S(1)}, bf16[16,192,128]{2,1,0:T(8,128)(2,1)}, u32[]{:S(2)}, u32[]{:S(2)}) collective-permute-start(bf16[16,192,128]{2,1,0:T(8,128)(2,1)S(1)} %all_to_all.10.a), channel_id=1, source_target_pairs={{0,1},{1,0},{2,3},{3,2},{4,5},{5,4},{6,7},{7,6},{8,9},{9,8},{10,11... | collective-permute-start | bytes 2359304 | tf_op jit(solution)/shard_map/ppermute | solution.py:56
  91.3 12.8 %collective-permute-start.18 = (bf16[16,192,128]{2,1,0:T(8,128)(2,1)}, bf16[16,192,128]{2,1,0:T(8,128)(2,1)}, u32[]{:S(2)}, u32[]{:S(2)}) collective-permute-start(bf16[16,192,128]{2,1,0:T(8,128)(2,1)} %copy-done.6), channel_id=1, source_target_pairs={{0,1},{1,0},{2,3},{3,2},{4,5},{5,4},{6,7},{7,6},{8,9},{9,8},{10,11... | collective-permute-start | bytes 2359304 | tf_op jit(solution)/shard_map/ppermute | solution.py:56
  91.4 12.7 %collective-permute-start.16 = (bf16[384,1024]{1,0:T(8,128)(2,1)}, bf16[384,1024]{1,0:T(8,128)(2,1)}, u32[]{:S(2)}, u32[]{:S(2)}) collective-permute-start(bf16[384,1024]{1,0:T(8,128)(2,1)} %copy-done.5), channel_id=1, source_target_pairs={{0,1},{1,0},{2,3},{3,2},{4,5},{5,4},{6,7},{7,6},{8,9},{9,8},{10,11... | collective-permute-start | bytes 2359304 | tf_op jit(solution)/shard_map/ppermute | solution.py:56
  91.8 25.0 %collective-permute-start.14 = (bf16[16,192,128]{2,1,0:T(8,128)(2,1)S(1)}, bf16[16,192,128]{2,1,0:T(8,128)(2,1)}, u32[]{:S(2)}, u32[]{:S(2)}) collective-permute-start(bf16[16,192,128]{2,1,0:T(8,128)(2,1)S(1)} %collective-permute-done.2.a), channel_id=1, source_target_pairs={{0,1},{1,0},{2,3},{3,2},{4,5},{5,4},{6,7},{7,6},{8,9},{9,8},{10,11... | collective-permute-start | bytes 2359304 | tf_op jit(solution)/shard_map/ppermute | solution.py:56
  91.9 24.9 %collective-permute-start.15 = (bf16[16,192,128]{2,1,0:T(8,128)(2,1)}, bf16[16,192,128]{2,1,0:T(8,128)(2,1)}, u32[]{:S(2)}, u32[]{:S(2)}) collective-permute-start(bf16[16,192,128]{2,1,0:T(8,128)(2,1)} %copy-done.3), channel_id=1, source_target_pairs={{0,1},{1,0},{2,3},{3,2},{4,5},{5,4},{6,7},{7,6},{8,9},{9,8},{10,11... | collective-permute-start | bytes 2359304 | tf_op jit(solution)/shard_map/ppermute | solution.py:56
  101.2 15.6 %copy-start.4 = (bf16[16,192,128]{2,1,0:T(8,128)(2,1)S(1)}, bf16[16,192,128]{2,1,0:T(8,128)(2,1)}, u32[]{:S(2)}) copy-start(bf16[16,192,128]{2,1,0:T(8,128)(2,1)} %copy-done.3) | copy-start | bytes 2359300
  101.2 15.2 %collective-permute-start.10 = (bf16[192,128]{1,0:T(8,128)(2,1)S(1)}, bf16[192,128]{1,0:T(8,128)(2,1)S(1)}, u32[]{:S(2)}, u32[]{:S(2)}) collective-permute-start(bf16[192,128]{1,0:T(8,128)(2,1)S(1)} %get-tuple-element.33.own), channel_id=1, source_target_pairs={{0,2},{2,0},{1,3},{3,1},{4,6},{6,4},{5,7},{7,5},{8,10},{10,8},{9,1... | collective-permute-start | bytes 147464 | tf_op jit(solution)/shard_map/ppermute | solution.py:56
  104.1 1.1 copy-start.7
  112.3 11.6 %collective-permute-start.11 = (bf16[192,128]{1,0:T(8,128)(2,1)S(1)}, bf16[192,128]{1,0:T(8,128)(2,1)S(1)}, u32[]{:S(2)}, u32[]{:S(2)}) collective-permute-start(bf16[192,128]{1,0:T(8,128)(2,1)S(1)} %get-tuple-element.33.own), channel_id=1, source_target_pairs={{0,1},{1,0},{2,3},{3,2},{4,5},{5,4},{6,7},{7,6},{8,9},{9,8},{10,11... | collective-permute-start | bytes 147464 | tf_op jit(solution)/shard_map/ppermute | solution.py:56
  116.3 7.7 %copy-start.2 = (bf16[1,768,1024]{2,1,0:T(8,128)(2,1)S(1)}, bf16[1,768,1024]{2,1,0:T(8,128)(2,1)}, u32[]{:S(2)}) copy-start(bf16[1,768,1024]{2,1,0:T(8,128)(2,1)} %param.5) | copy-start | bytes 4718596
  116.3 7.6 %collective-permute-start.13 = (f32[8,128]{1,0:T(8,128)S(1)}, f32[8,128]{1,0:T(8,128)S(1)}, u32[]{:S(2)}, u32[]{:S(2)}) collective-permute-start(f32[8,128]{1,0:T(8,128)S(1)} %get-tuple-element.34.loss), channel_id=1, source_target_pairs={{0,1},{1,0},{2,3},{3,2},{4,5},{5,4},{6,7},{7,6},{8,9},{9,8},{10,11... | collective-permute-start | bytes 12296 | tf_op jit(solution)/shard_map/ppermute | solution.py:56
  116.4 7.6 %collective-permute-start.12 = (bf16[192,128]{1,0:T(8,128)(2,1)S(1)}, bf16[192,128]{1,0:T(8,128)(2,1)S(1)}, u32[]{:S(2)}, u32[]{:S(2)}) collective-permute-start(bf16[192,128]{1,0:T(8,128)(2,1)S(1)} %collective-permute-done.10.beside), channel_id=1, source_target_pairs={{0,1},{1,0},{2,3},{3,2},{4,5},{5,4},{6,7},{7,6},{8,9},{9,8},{10,11... | collective-permute-start | bytes 147464 | tf_op jit(solution)/shard_map/ppermute | solution.py:56
  116.8 9.1 %copy-start.1 = (bf16[1,1024,128]{2,1,0:T(8,128)(2,1)S(1)}, bf16[1,1024,128]{2,1,0:T(8,128)(2,1)}, u32[]{:S(2)}) copy-start(bf16[1,1024,128]{2,1,0:T(8,128)(2,1)} %param.7) | copy-start | bytes 786436
where the time goes:
time: 127 us; the launch traced here: 126 us
  Pallas kernels  42.8 us (34%)
  starting transfers between devices  26.4 us (21%)
  waiting for transfers between devices  25.1 us (20%)
  blocking collectives  24.2 us (19%)
  local copies, waits for them, and re-layouts  4.34 us (3%)
  matrix products  1.97 us (2%)
    pallas_call x11, Pallas kernels, call(): pl.pallas_call(kernel, in_specs=specs, out_specs=out_specs, out_shape=out...  42.8 us
    all_to_all x1, blocking collectives, in_coset(): lax.all_to_all(blocks, AXES, 0, 0, axis_index_groups=COSETS, tiled=True)  24.2 us
    ppermute x13, starting transfers between devices, swapped(): return lax.ppermute(array, axis, SWAP)  16.6 us
    ppermute x6, waiting for transfers between devices, sent(): return lax.ppermute(array, AXES, toward(shift, back))  12.6 us
    all_to_all x1, waiting for transfers between devices, in_coset(): lax.all_to_all(blocks, AXES, 0, 0, axis_index_groups=COSETS, tiled=True)  8.59 us
    all_to_all x1, starting transfers between devices, in_coset(): lax.all_to_all(blocks, AXES, 0, 0, axis_index_groups=COSETS, tiled=True)  5.47 us
    ppermute x6, starting transfers between devices, sent(): return lax.ppermute(array, AXES, toward(shift, back))  4.31 us
    ppermute x13, waiting for transfers between devices, swapped(): return lax.ppermute(array, axis, SWAP)  3.9 us
  transfers between devices with their start and end apart: 20, of which 5 were waited for; matrix products, arithmetic and copies ran while one was open for 2% of the time, Pallas kernels for 20%

commit v1 on v0

v1 whole, which is shorter than its diff:
```python
import functools
import itertools

import jax
import jax.numpy as jnp
from jax import lax
from jax.experimental import pallas as pl
from jax.experimental.pallas import tpu as pltpu
from jax.sharding import Mesh
from jax.sharding import PartitionSpec as P

AXES = ("x", "z", "yh", "yl", "c")
LAYER = ("x", "z", "yh")
WIDTH = ("yl", "c")
SWAP = [(0, 1), (1, 0)]
RING = 4
EXTRA = 16
INTERPRET = False

sparsity = 8.0
f32, bf16 = jnp.float32, jnp.bfloat16


def flat(x, z, y, c):
    return ((x % RING * RING + z % RING) * RING + y % RING) * 2 + c


def toward(shift, back=False):
    pairs = []
    for x, z, y, c in itertools.product(range(RING), range(RING), range(RING), range(2)):
        if c == 0:
            there = {1: (x + 1, z, y), 3: (x - 1, z, y), 2: (x, z, y + 1)}[shift]
        else:
            there = {1: (x, z + 1, y), 3: (x, z - 1, y), 2: (x, z, y - 1)}[shift]
        pair = (flat(x, z, y, c), flat(*there, c))
        pairs.append(pair[::-1] if back else pair)
    return pairs


COSETS = [
    [flat(x, f - x - 2 * yl, 2 * yh + yl, c) for x in range(RING) for yh in range(2) for yl in range(2)]
    for f in range(RING)
    for c in range(2)
]


def sent(array, shift, back=False):
    return lax.ppermute(array, AXES, toward(shift, back))


def in_coset(blocks):
    return lax.all_to_all(blocks, AXES, 0, 0, axis_index_groups=COSETS, tiled=True)


def swapped(array, axis):
    return lax.ppermute(array, axis, SWAP)


def halves(array, axis, dim=0):
    half = array.shape[dim] // 2
    own = lax.axis_index(axis)
    mine = lax.dynamic_slice_in_dim(array, own * half, half, dim)
    theirs = lax.dynamic_slice_in_dim(array, (1 - own) * half, half, dim)
    return mine, theirs


def placement():
    x, side = lax.axis_index("x"), lax.axis_index("yl")
    coset = lax.rem(x + lax.axis_index("z") + 2 * side, RING)
    tile = 4 * x + 2 * lax.axis_index("yh") + side
    return coset, lax.axis_index(LAYER), lax.axis_index("c"), side, tile


def pair_of(place, offset, turn, x):
    return RING * x + lax.rem(place[0] + offset + 2 * turn + RING - x, RING)


ORDER = tuple(itertools.product(range(2), range(RING)))
CHIP = pl.BlockSpec(memory_space=pltpu.VMEM)
SCALARS = pl.BlockSpec(memory_space=pltpu.SMEM)
FAR = pl.BlockSpec(memory_space=pltpu.HBM)
ANY = pl.BlockSpec(memory_space=pl.ANY)


def near(array):
    return array if INTERPRET else pltpu.with_memory_space_constraint(array, pltpu.VMEM)


def far(array):
    return array if INTERPRET else pltpu.with_memory_space_constraint(array, pltpu.HBM)


def near_out(shape, kind):
    return jax.ShapeDtypeStruct(shape, kind) if INTERPRET else pltpu.VMEM(shape, kind)


def call(kernel, args, specs, outs, out_specs, scratch=(), flops=0, traffic=0, mib=16, **more):
    return pl.pallas_call(
        kernel,
        in_specs=specs,
        out_specs=out_specs,
        out_shape=outs,
        scratch_shapes=list(scratch),
        interpret=INTERPRET,
        compiler_params=pltpu.CompilerParams(vmem_limit_bytes=mib << 20),
        cost_estimate=pl.CostEstimate(flops=flops, bytes_accessed=traffic, transcendentals=0),
        **more,
    )(*args)


def load_kernel(source, out, sem):
    place = placement()
    depth = source.shape[1] // 2
    for pair, yh in itertools.product(range(source.shape[0]), range(2)):
        rows = slice(yh * depth, (yh + 1) * depth)
        used = 2 * pair + yh <= place[1]

        @pl.when(used)
        def _():
            pltpu.make_async_copy(source.at[pair, rows, :], out.at[pair, rows, :], sem.at[pair, yh]).start()

        @pl.when(jnp.logical_not(used))
        def _():
            out[pair, rows, :] = jnp.zeros((depth, source.shape[2]), out.dtype)

    for pair, yh in itertools.product(range(source.shape[0]), range(2)):
        rows = slice(yh * depth, (yh + 1) * depth)

        @pl.when(2 * pair + yh <= place[1])
        def _():
            pltpu.make_async_copy(source.at[pair, rows, :], out.at[pair, rows, :], sem.at[pair, yh]).wait()


def loaded(array):
    return call(
        load_kernel,
        [far(array)],
        [FAR],
        near_out(array.shape, array.dtype),
        CHIP,
        [pltpu.SemaphoreType.DMA((array.shape[0], 2))],
        flops=array.size * 400,
        traffic=array.size * 4,
        mib=1,
    )


def quarters(turn, quarter):
    first = slice(turn * quarter, (turn + 1) * quarter)
    second = slice((1 - turn) * quarter, (2 - turn) * quarter)
    return first, second


def lay_out_pair(a, b, lhs):
    quarter, latent = a.shape[1:]
    for i, (turn, x) in enumerate(ORDER):
        rows_a, rows_b = quarters(turn, quarter)
        for yh in range(2):
            at = 4 * x + 2 * yh
            lanes = slice((2 * i + yh) * latent, (2 * i + yh + 1) * latent)
            lhs[rows_a, lanes] = a[at + turn]
            lhs[rows_b, lanes] = b[at + 1 - turn]


def lay_out(place, offset, sides, lhs):
    half = lhs.shape[0] // len(sides)
    latent = sides[0][0].shape[2]
    for i, (turn, x) in enumerate(ORDER):
        rows_a, rows_b = quarters(turn, half // 2)
        for yh in range(2):
            layer = 2 * pair_of(place, offset, turn, x) + yh
            at = 4 * x + 2 * yh
            lanes = slice((2 * i + yh) * latent, (2 * i + yh + 1) * latent)

            @pl.when(layer <= place[1])
            def _():
                for side, (a, b) in enumerate(sides):
                    block = lhs.at[side * half : (side + 1) * half]
                    block[rows_a, lanes] = a[at + turn]
                    block[rows_b, lanes] = b[at + 1 - turn]

            @pl.when(layer > place[1])
            def _():
                lhs[:, lanes] = jnp.zeros((lhs.shape[0], latent), lhs.dtype)


def lay_out_block(block, lhs):
    quarter, latent = block.shape[1:]
    for q, x, yh in itertools.product(range(2), range(RING), range(2)):
        rows = slice(q * quarter, (q + 1) * quarter)
        lanes = slice((2 * x + yh) * latent, (2 * x + yh + 1) * latent)
        lhs[rows, lanes] = block[4 * x + 2 * yh + q]


def block_product(place, shift, lhs, source, cols):
    quarter = lhs.shape[0] // 2
    parts = []
    for q in range(2):
        pairs = [pair_of(place, shift, q, x) for x in range(RING)]
        rhs = jnp.concatenate([source[pair, :, cols] for pair in pairs], axis=0)
        rows = slice(q * quarter, (q + 1) * quarter)
        parts.append(jnp.dot(lhs[rows, :], rhs, preferred_element_type=f32))
    return jnp.concatenate(parts, axis=0)


def column_steps(columns):
    step = min(512, columns)
    for start in range(0, columns, step):
        yield start, slice(start, start + step)


def home_kernel(block, w, v, total, lhs):
    place = placement()
    lay_out_block(block, lhs)
    columns = w.shape[2]
    for side, source in enumerate((w, v)):
        for start, cols in column_steps(columns):
            both = slice(side * columns + start, side * columns + cols.stop)
            total[:, both] = block_product(place, 0, lhs, source, cols)


def rebuilt_home(block, w, v):
    quarter, latent = block.shape[1:]
    half = 2 * quarter
    depth, columns = w.shape[1:]
    args = [near(t) for t in (block, w, v)]
    scratch = [pltpu.VMEM((half, 8 * latent), bf16)]
    out = near_out((half, 2 * columns), f32)
    flops = half * 2 * columns * 8 * depth
    return call(home_kernel, args, [CHIP] * 3, out, CHIP, scratch, flops, 1 << 20)


def forward_kernel(tokens, two, a, b, w, v, before, outputs, other, *rest):
    place = placement()
    signal, signal_other, squares, lhs, lhs_two, wanted, wanted_other, sems = rest
    half = 2 * a.shape[1]
    columns = w.shape[2]
    rows = pl.ds(pl.multiple_of(place[2] * half, 16), half)
    copy = pltpu.make_async_copy(outputs.at[rows, :], wanted, sems.at[0])
    copy.start()
    copy_other = pltpu.make_async_copy(other, wanted_other, sems.at[1])
    copy_other.start()
    lay_out_block(two, lhs_two)
    lay_out_pair(a, b, lhs)
    pairs = [pair_of(place, 1, turn, x) for turn, x in ORDER]
    carry = jnp.zeros((16, 128), f32)
    sides = ((w, wanted, signal), (v, wanted_other, signal_other))
    for side, (source, target, out) in enumerate(sides):
        for start, cols in column_steps(columns):
            both = slice(side * columns + start, side * columns + cols.stop)
            rhs = jnp.concatenate([source[pair, :, cols] for pair in pairs], axis=0)
            product = jnp.dot(lhs[...], rhs, preferred_element_type=f32)
            product = product + block_product(place, 2, lhs_two, source, cols)
            if side == 0 and start == 0:
                copy.wait()
                copy_other.wait()
            misfit = product + before[:, both] - target[:, cols].astype(f32)
            out[:, cols] = (misfit * (1.0 / tokens)).astype(bf16)
            square = misfit * misfit
            square = jnp.sum(square.reshape(-1, 16, square.shape[1]), axis=0)
            for lane in range(0, square.shape[1], 128):
                carry = carry + square[:, lane : lane + 128]
    squares[...] = carry


def forward(tokens, two, a, b, w, v, before, outputs, wanted_other):
    quarter, latent = a.shape[1:]
    half = 2 * quarter
    depth, columns = w.shape[1:]
    args = [near(t) for t in (two, a, b, w, v, before)] + [far(outputs), wanted_other]
    specs = [CHIP] * 6 + [FAR, ANY]
    scratch = [pltpu.VMEM((half, 16 * latent), bf16), pltpu.VMEM((half, 8 * latent), bf16)]
    scratch += [pltpu.VMEM((half, columns), bf16)] * 2 + [pltpu.SemaphoreType.DMA((2,))]
    outs = (near_out((half, columns), bf16), near_out((half, columns), bf16), near_out((16, 128), f32))
    flops = 3 * half * 2 * columns * 8 * depth
    kernel = functools.partial(forward_kernel, tokens)
    return call(kernel, args, specs, outs, (CHIP,) * 3, scratch, flops, 1 << 20)


def write_notes(squares, fired, *blocks):
    quarter, latent = blocks[0].shape[1] - EXTRA, blocks[0].shape[2]
    loss = 0.5 * jnp.sum(squares[...]) + sparsity * jnp.sum(fired[...])
    loss = jnp.full((8, latent), loss, f32)
    high = loss.astype(bf16).astype(f32)
    note = jnp.concatenate([high, loss - high], axis=0).astype(bf16)
    for block in blocks:
        for tile in range(block.shape[0]):
            block[tile, quarter:, :] = note


NT = (((1,), (1,)), ((), ()))


def terms_kernel(offset, signal, signal_other, w, v, squares, fired, a, b):
    place = placement()
    quarter, latent = a.shape[1] - EXTRA, a.shape[2]
    write_notes(squares, fired, a, b)
    for turn in range(2):
        pairs = [pair_of(place, offset, turn, x) for x in range(RING)]
        rows_a, rows_b = quarters(turn, quarter)
        term = None
        for left, right in ((signal, w), (signal_other, v)):
            rhs = jnp.concatenate([right[pair] for pair in pairs], axis=0)
            part = lax.dot_general(left[...], rhs, NT, preferred_element_type=f32)
            term = part if term is None else term + part
        term = term.astype(bf16)
        for x, yh in itertools.product(range(RING), range(2)):
            at = 4 * x + 2 * yh
            lanes = slice((2 * x + yh) * latent, (2 * x + yh + 1) * latent)
            a[at + turn, :quarter, :] = term[rows_a, lanes]
            b[at + 1 - turn, :quarter, :] = term[rows_b, lanes]


def terms_for(offset, signal, signal_other, w, v, squares, fired):
    half, columns = signal.shape
    depth = w.shape[1]
    latent = depth // 2
    args = [near(t) for t in (signal, signal_other, w, v, squares, fired)]
    out = near_out((16, half // 2 + EXTRA, latent), bf16)
    flops = 2 * half * 2 * columns * 8 * depth
    kernel = functools.partial(terms_kernel, offset)
    return call(kernel, args, [CHIP] * 6, (out, out), (CHIP, CHIP), (), flops, 1 << 20)


def gradient_kernel(offset, a, b, a_other, b_other, signal, signal_other, *rest):
    place = placement()
    out, lhs, rhs, held, sems, sems_in = rest[-6:]
    half = signal.shape[0]
    depth = held.shape[1]
    incoming = pltpu.make_async_copy(signal, rhs.at[:half, :], sems_in.at[0])
    incoming.start()
    incoming_other = pltpu.make_async_copy(signal_other, rhs.at[half:, :], sems_in.at[1])
    incoming_other.start()
    lay_out(place, offset, [(a, b), (a_other, b_other)], lhs)
    incoming.wait()
    incoming_other.wait()
    contract = (((0,), (0,)), ((), ()))
    copies = []
    for i in range(0, len(ORDER), 2):
        left = lhs[:, i * depth : (i + 2) * depth]
        product = lax.dot_general(left, rhs[...], contract, preferred_element_type=f32).astype(bf16)
        for j in range(2):
            held[i + j] = product[j * depth : (j + 1) * depth]
            pair = pair_of(place, offset, *ORDER[i + j])
            copy = pltpu.make_async_copy(held.at[i + j], out.at[pair], sems.at[i + j])
            copy.start()
            copies.append(copy)
    for copy in copies:
        copy.wait()


def gradient(offset, a, b, a_other, b_other, signal, signal_other, so_far=None):
    latent = a.shape[2]
    half, columns = signal.shape
    args = [near(t) for t in (a, b, a_other, b_other)] + [signal, far(signal_other)]
    specs = [CHIP] * 4 + [ANY, FAR]
    aliases = {}
    if so_far is not None:
        aliases = {len(args): 0}
        args.append(so_far)
        specs.append(FAR)
    scratch = [
        pltpu.VMEM((2 * half, 16 * latent), bf16),
        pltpu.VMEM((2 * half, columns), bf16),
        pltpu.VMEM((len(ORDER), 2 * latent, columns), bf16),
        pltpu.SemaphoreType.DMA((len(ORDER),)),
        pltpu.SemaphoreType.DMA((2,)),
    ]
    out = jax.ShapeDtypeStruct((RING * RING, 2 * latent, columns), bf16)
    flops = 2 * 2 * half * columns * 16 * latent
    kernel = functools.partial(gradient_kernel, offset)
    return call(kernel, args, specs, out, FAR, scratch, flops, 1 << 20, mib=20, input_output_aliases=aliases)


def sum_kernel(own, one, two, three, out):
    quarter = own.shape[1] - EXTRA
    parts = (own, one, two, three)
    for tile in range(own.shape[0]):
        total = functools.reduce(lambda s, p: s + p, [p[tile, :quarter, :].astype(f32) for p in parts])
        out[tile, :quarter, :] = total.astype(bf16)
        row = lax.broadcasted_iota(jnp.int32, (EXTRA, own.shape[2]), 0)
        note = jnp.zeros((EXTRA, own.shape[2]), f32)
        for i, part in enumerate(parts):
            heard = part[tile, quarter:, :].astype(f32)
            high = jnp.broadcast_to(heard[:1], heard.shape)
            low = jnp.broadcast_to(heard[8:9], heard.shape)
            note = jnp.where(row == 2 * i, high, jnp.where(row == 2 * i + 1, low, note))
        out[tile, quarter:, :] = note.astype(bf16)


def summed(*parts):
    args = [near(part) for part in parts]
    out = jax.ShapeDtypeStruct(parts[0].shape, bf16)
    return call(sum_kernel, args, [CHIP] * 4, out, CHIP, (), 1 << 20, 1 << 20, mib=4)


def encode_kernel(flip, inputs, weights, *rest):
    place = placement()
    out, rows_here, weights_here, sems = rest[-4:]
    half = out.shape[0]
    which = 1 - place[2] if flip else place[2]
    rows = pl.ds(pl.multiple_of(which * half, 16), half)
    copies = (
        pltpu.make_async_copy(inputs.at[rows, :], rows_here, sems.at[0]),
        pltpu.make_async_copy(weights, weights_here, sems.at[1]),
    )
    for copy in copies:
        copy.start()
    for copy in copies:
        copy.wait()
    out[...] = jnp.dot(rows_here[...], weights_here[...], preferred_element_type=f32)
    if not flip:

        @pl.when(place[3] == 0)
        def _():
            out[...] += rest[0][...]


def encoded(flip, inputs, weights, bias):
    tokens, columns = inputs.shape
    latent = weights.shape[1]
    scratch = [
        pltpu.VMEM((tokens // 2, columns), bf16),
        pltpu.VMEM((columns, latent), bf16),
        pltpu.SemaphoreType.DMA((2,)),
    ]
    out = near_out((tokens // 2, latent), f32)
    kernel = functools.partial(encode_kernel, flip)
    args = [far(inputs), far(weights)] + ([] if flip else [bias])
    return call(kernel, args, [FAR, FAR, CHIP][: len(args)], out, CHIP, scratch, 1 << 20, 1 << 20, mib=4)


def fire_kernel(mine, heard, fired, blocks):
    place = placement()
    quarter = heard.shape[0]
    rows = pl.ds(pl.multiple_of(place[3] * quarter, 16), quarter)
    value = mine[rows, :] + heard[...]
    active = jnp.maximum(value, 0.0)
    fired[...] = jnp.sum(active.reshape(-1, 8, active.shape[1]), axis=0)
    firing = active.astype(bf16)
    for tile in range(blocks.shape[0]):
        blocks[tile] = firing


def fire(mine, heard):
    quarter, latent = heard.shape
    args = [near(mine), near(heard)]
    outs = (
        near_out((8, latent), f32),
        near_out((16, quarter, latent), bf16),
    )
    return call(fire_kernel, args, [CHIP] * 2, outs, (CHIP,) * 2, (), 1 << 20, 1 << 20, mib=4)


def delta_kernel(tokens, arrived, firing, delta):
    place = placement()
    quarter, latent = firing.shape[1:]
    total = arrived[0, :quarter, :].astype(f32)
    for tile in range(1, arrived.shape[0]):
        total = total + arrived[tile, :quarter, :].astype(f32)
    positive = firing[place[4]].astype(f32) > 0
    total = jnp.where(positive, total + sparsity / tokens, 0.0)
    delta[:quarter, :] = total.astype(bf16)
    losses = []
    for tile in range(arrived.shape[0]):
        notes = arrived[tile, quarter:, :].astype(f32)
        losses += [notes[2 * i : 2 * i + 1] + notes[2 * i + 1 : 2 * i + 2] for i in range(RING)]
    unit = jnp.maximum(functools.reduce(jnp.maximum, losses), 1e-30)
    whole = functools.reduce(lambda p, q: p + q, [jnp.round(value / unit * 65536.0) for value in losses])
    loss = jnp.broadcast_to(whole * (unit / 65536.0), (8, latent))
    high = loss.astype(bf16).astype(f32)
    delta[quarter:, :] = jnp.concatenate([high, loss - high], axis=0).astype(bf16)


def delta_of(arrived, firing, tokens):
    quarter, latent = firing.shape[1:]
    args = [near(arrived), near(firing)]
    out = near_out((quarter + EXTRA, latent), bf16)
    kernel = functools.partial(delta_kernel, tokens)
    return call(kernel, args, [CHIP] * 2, out, CHIP, (), 1 << 20, 1 << 20, mib=8)


def finish_kernel(size, inputs, own, beside, opposite, last, encoder, bias, mean, delta):
    place = placement()
    quarter = own.shape[0] - EXTRA
    core, side = place[2], place[3]
    parts = ((own, core, side), (beside, core, 1 - side), (opposite, 1 - core, side), (last, 1 - core, 1 - side))
    for part, c, y in parts:
        delta[pl.ds(pl.multiple_of((2 * c + y) * quarter, 16), quarter), :] = part[:quarter, :]
    contract = (((0,), (0,)), ((), ()))
    product = lax.dot_general(inputs[...], delta[...], contract, preferred_element_type=f32)
    encoder[...] = product.astype(bf16)
    bias[...] = jnp.sum(delta[...].astype(f32), axis=0, keepdims=True)
    losses = []
    for part in (own, opposite):
        notes = part[quarter:, :].astype(f32)
        losses.append(jnp.max(notes[:8] + notes[8:]))
    mean[0, 0] = (losses[0] + losses[1]) / size


def finished(size, inputs, *parts):
    tokens, columns = inputs.shape
    latent = parts[0].shape[1]
    args = [near(t) for t in (inputs, *parts)]
    outs = (
        jax.ShapeDtypeStruct((columns, latent), bf16),
        jax.ShapeDtypeStruct((1, latent), f32),
        jax.ShapeDtypeStruct((1, 1), f32),
    )
    scratch = [pltpu.VMEM((tokens, latent), bf16)]
    kernel = functools.partial(finish_kernel, size)
    return call(kernel, args, [CHIP] * 5, outs, (CHIP, CHIP, SCALARS), scratch, 1 << 20, 1 << 20, mib=8)


def whole_step(mlp_inputs, mlp_outputs, encoders, encoder_bias, decoders):
    inputs = mlp_inputs[0]
    tokens = inputs.shape[0]
    width = inputs.shape[1] * lax.axis_size(WIDTH)
    layers = lax.axis_size(LAYER)
    latent = encoders.shape[2]
    core = lax.axis_index("c")

    theirs = encoded(True, inputs, encoders[0], encoder_bias)
    heard = swapped(theirs, "c")
    mine = encoded(False, inputs, encoders[0], encoder_bias)
    weights = decoders[0].reshape(layers // 2, 2 * latent, -1)
    outputs = mlp_outputs[0]
    heard, weights, outputs = lax.optimization_barrier((heard, weights, outputs))
    partial = mine + heard
    weights_other = swapped(weights, "c")
    _, theirs = halves(partial, "yl")
    half = tokens // 2
    wanted_sent = lax.dynamic_slice_in_dim(outputs, (1 - core) * half, half, 0)
    wanted_other = swapped(wanted_sent, "c")
    heard = swapped(theirs, "yl")
    fired, blocks = fire(partial, heard)

    own = in_coset(blocks)
    two = sent(own, 2)
    one = sent(own, 1)
    three = sent(own, 3)
    own_other = swapped(own, "c")
    two_other = swapped(two, "c")
    one_other = swapped(one, "c")
    three_other = swapped(three, "c")

    weights = loaded(weights)
    weights_other = loaded(weights_other)
    total = rebuilt_home(own, weights, weights_other)
    signal, signal_other, squares = forward(
        tokens, two, three, one, weights, weights_other, total, outputs, wanted_other
    )
    signal_here = swapped(signal_other, "c")

    rest = (signal, signal_other, weights, weights_other, squares, fired)
    at_home, to_two = terms_for(0, *rest)
    from_two = sent(to_two, 2, back=True)
    to_three, to_one = terms_for(1, *rest)
    from_one = sent(to_one, 1, back=True)
    from_three = sent(to_three, 3, back=True)
    signals = (signal, signal_here)
    grad_decoder = gradient(0, own, two, own_other, two_other, *signals)
    arrived = in_coset(summed(at_home, from_one, from_two, from_three))
    grad_decoder = gradient(1, three, one, three_other, one_other, *signals, grad_decoder)

    delta = delta_of(arrived, own, tokens)
    beside = swapped(delta, "yl")
    last = lax.ppermute(delta, WIDTH, [(0, 3), (1, 2), (2, 1), (3, 0)])
    opposite = swapped(delta, "c")
    size = float(tokens * width * layers)
    grad_encoder, grad_bias, loss_mean = finished(
        size, inputs, delta, beside, opposite, last
    )
    return (loss_mean[0, 0], grad_encoder[None], grad_bias, grad_decoder.reshape(decoders.shape))


def solution(mesh):
    finer = Mesh(mesh.devices.reshape(4, 4, 2, 2, 2), AXES)
    placed = (
        P(LAYER, None, WIDTH),
        P(LAYER, None, WIDTH),
        P(LAYER, WIDTH, None),
        P(LAYER, None),
        P(LAYER, None, None, WIDTH),
    )
    return jax.shard_map(
        whole_step,
        mesh=finer,
        in_specs=placed,
        out_specs=(P(), P(LAYER, WIDTH, None), P(LAYER, None), P(LAYER, None, None, WIDTH)),
        check_vma=False,
    )
```

time: 127 us -> 117 us (0.921)
  blocking collectives: 24.2 us -> 0 us
  starting transfers between devices: 26.4 us -> 43.5 us
  Pallas kernels: 42.8 us -> 40.2 us
  waiting for transfers between devices: 25.1 us -> 27.6 us
  matrix products: 1.97 us -> 0 us
    all_to_all x1 -> x0, blocking collectives: 24.2 us -> none  [in_coset(): lax.all_to_all(blocks, AXES, 0, 0, axis_index_groups=COSETS, tiled=True)]
    all_to_all x1 -> x2, starting transfers between devices: 5.47 us -> 14.9 us  [in_coset(): lax.all_to_all(blocks, AXES, 0, 0, axis_index_groups=COSETS, tiled=True)]
    ppermute x13 -> x11, starting transfers between devices: 16.6 us -> 24.6 us  [swapped(): return lax.ppermute(array, axis, SWAP)]
    all_to_all x1 -> x2, waiting for transfers between devices: 8.59 us -> 11.8 us  [in_coset(): lax.all_to_all(blocks, AXES, 0, 0, axis_index_groups=COSETS, tiled=True)]
    pallas_call x11 -> x14, Pallas kernels: 42.8 us -> 40.2 us  [call(): pl.pallas_call(kernel, in_specs=specs, out_specs=out_specs, out_shape=out...]
    dot_general x1 -> x0, matrix products: 1.97 us -> none  [whole_step(): partial = jnp.dot(inputs, encoders[0], preferred_element_type=f32)]
    unnamed x18 -> x12, local copies, waits for them, and re-layouts: 2.1 us -> 2.93 us
    ppermute x13 -> x11, waiting for transfers between devices: 3.9 us -> 3.91 us  [swapped(): return lax.ppermute(array, axis, SWAP)]
  transfers between devices with their start and end apart: 20 -> 20, of which waited for: 5 -> 9; matrix products, arithmetic and copies ran while one was open for 2% -> 1% of each run, Pallas kernels for 20% -> 23%
where the time goes in v1:
time: 117 us
  starting transfers between devices  43.5 us (37%)
  Pallas kernels  40.2 us (34%)
  waiting for transfers between devices  27.6 us (24%)
  local copies, waits for them, and re-layouts  4.14 us (4%)
    pallas_call x14, Pallas kernels, call(): pl.pallas_call(kernel, in_specs=specs, out_specs=out_specs, out_shape=out...  40.2 us
    ppermute x11, starting transfers between devices, swapped(): return lax.ppermute(array, axis, SWAP)  24.6 us
    all_to_all x2, starting transfers between devices, in_coset(): lax.all_to_all(blocks, AXES, 0, 0, axis_index_groups=COSETS, tiled=True)  14.9 us
    ppermute x6, waiting for transfers between devices, sent(): return lax.ppermute(array, AXES, toward(shift, back))  12 us
    all_to_all x2, waiting for transfers between devices, in_coset(): lax.all_to_all(blocks, AXES, 0, 0, axis_index_groups=COSETS, tiled=True)  11.8 us
    ppermute x11, waiting for transfers between devices, swapped(): return lax.ppermute(array, axis, SWAP)  3.91 us
    ppermute x6, starting transfers between devices, sent(): return lax.ppermute(array, AXES, toward(shift, back))  3.88 us
    unnamed x12, local copies, waits for them, and re-layouts  2.93 us
  transfers between devices with their start and end apart: 20, of which 9 were waited for; matrix products, arithmetic and copies ran while one was open for 1% of the time, Pallas kernels for 23%

profile of v1, /device:TPU:1, one launch (start us, length us, event | category | flops | bytes accessed | tf_op | source)
XLA Modules:
  0.0 116.6 jit_solution(5352227961177650727)
XLA Ops:
  0.6 1.6 %shard_map.85 = f32[384,128]{1,0:T(8,128)S(1)} custom-call(bf16[768,1024]{1,0:T(8,128)(2,1)} %bitcast.7, bf16[1024,128]{1,0:T(8,128)(2,1)} %bitcast.15), custom_call_target="tpu_custom_call" | custom-call | flops 1048576 | bytes 1048576 | tf_op jit(solution)/shard_map/pallas_call | solution.py:98
  2.2 1.5 %collective-permute-start = (f32[384,128]{1,0:T(8,128)S(1)}, f32[384,128]{1,0:T(8,128)S(1)}, u32[]{:S(2)}, u32[]{:S(2)}) collective-permute-start(f32[384,128]{1,0:T(8,128)S(1)} %shard_map.85), channel_id=1, source_target_pairs={{0,1},{1,0},{2,3},{3,2},{4,5},{5,4},{6,7},{7,6},{8,9},{9,8},{10,11... | collective-permute-start | bytes 589832 | tf_op jit(solution)/shard_map/ppermute | solution.py:56
  3.7 1.1 collective-permute-done
  4.8 0.4 collective-permute-start.5
  5.1 0.0 copy-start.5
  5.1 0.7 copy-done.5
  5.8 1.6 %shard_map.84 = f32[384,128]{1,0:T(8,128)S(1)} custom-call(bf16[768,1024]{1,0:T(8,128)(2,1)} %bitcast.8, bf16[1024,128]{1,0:T(8,128)(2,1)} %bitcast.16, f32[1,128]{1,0:T(1,128)S(1)} %copy-done.5), custom_call_target="tpu_custom_call" | custom-call | flops 1048576 | bytes 1048576 | tf_op jit(solution)/shard_map/pallas_call | solution.py:98
  7.4 1.5 %collective-permute-start.1 = (f32[192,128]{1,0:T(8,128)S(1)}, f32[192,128]{1,0:T(8,128)S(1)}, u32[]{:S(2)}, u32[]{:S(2)}) collective-permute-start(f32[192,128]{1,0:T(8,128)S(1)} %constant_dynamic-slice_fusion.1), channel_id=1, source_target_pairs={{0,2},{2,0},{1,3},{3,1},{4,6},{6,4},{5,7},{7,5},{8,10},{10,8},{9,1... | collective-permute-start | bytes 294920 | tf_op jit(solution)/shard_map/ppermute | solution.py:56
  8.9 2.8 %collective-permute-done.1.heard = f32[192,128]{1,0:T(8,128)S(1)} collective-permute-done((f32[192,128]{1,0:T(8,128)S(1)}, f32[192,128]{1,0:T(8,128)S(1)}, u32[]{:S(2)}, u32[]{:S(2)}) %collective-permute-start.1) | collective-permute-done | bytes 98336 | tf_op jit(solution)/shard_map/ppermute | solution.py:56
  11.7 1.0 shard_map.86
  12.7 10.2 %all-to-all-start = ((bf16[16,192,128]{2,1,0:T(8,128)(2,1)}), bf16[16,192,128]{2,1,0:T(8,128)(2,1)S(1)}, u32[]{:S(2)}, u32[]{:S(2)}) async-start(bf16[16,192,128]{2,1,0:T(8,128)(2,1)} %get-tuple-element.20), calls=%async_computation | async-start | bytes 1572864 | tf_op jit(solution)/shard_map/all_to_all | solution.py:52
  22.9 1.2 %constant_dynamic-slice_fusion = bf16[384,1024]{1,0:T(8,128)(2,1)S(1)} fusion(bf16[768,1024]{1,0:T(8,128)(2,1)} %bitcast.13, s32[]{:T(128)S(6)} %select_n.7), kind=kLoop, calls=%fused_computation | loop fusion | bytes 1572868 | tf_op jit(solution)/shard_map/dynamic_slice | solution.py:533
  24.1 1.4 %collective-permute-start.6 = (bf16[384,1024]{1,0:T(8,128)(2,1)S(1)}, bf16[384,1024]{1,0:T(8,128)(2,1)S(1)}, u32[]{:S(2)}, u32[]{:S(2)}) collective-permute-start(bf16[384,1024]{1,0:T(8,128)(2,1)S(1)} %constant_dynamic-slice_fusion), channel_id=1, source_target_pairs={{0,1},{1,0},{2,3},{3,2},{4,5},{5,4},{6,7},{7,6},{8,9},{9,8},{10,11... | collective-permute-start | bytes 2359304 | tf_op jit(solution)/shard_map/ppermute | solution.py:56
  25.4 11.8 %all-to-all-done.block.firing.a = bf16[16,192,128]{2,1,0:T(8,128)(2,1)S(1)} async-done(((bf16[16,192,128]{2,1,0:T(8,128)(2,1)}), bf16[16,192,128]{2,1,0:T(8,128)(2,1)S(1)}, u32[]{:S(2)}, u32[]{:S(2)}) %all-to-all-start) | async-done | bytes 786464 | tf_op jit(solution)/shard_map/all_to_all | solution.py:52
  37.2 0.2 collective-permute-start.2
  37.4 1.8 %collective-permute-start.3 = (bf16[16,192,128]{2,1,0:T(8,128)(2,1)S(1)}, bf16[16,192,128]{2,1,0:T(8,128)(2,1)S(1)}, u32[]{:S(2)}, u32[]{:S(2)}) collective-permute-start(bf16[16,192,128]{2,1,0:T(8,128)(2,1)S(1)} %all-to-all-done.block.firing.a), channel_id=1, source_target_pairs={{0,96},{1,25},{2,98},{3,27},{4,100},{5,29},{6,102},{7,31},{8,104},... | collective-permute-start | bytes 2359304 | tf_op jit(solution)/shard_map/ppermute | solution.py:48
  39.2 0.0 collective-permute-start.4
  39.2 1.2 %shard_map.87.w = bf16[16,256,1024]{2,1,0:T(8,128)(2,1)S(1)} custom-call(bf16[16,256,1024]{2,1,0:T(8,128)(2,1)} %bitcast.12), custom_call_target="tpu_custom_call" | custom-call | flops 1677721600 | bytes 16777216 | tf_op jit(solution)/shard_map/pallas_call | solution.py:98
  40.4 0.0 collective-permute-done.5.source
  40.4 1.3 %shard_map.88.v = bf16[16,256,1024]{2,1,0:T(8,128)(2,1)S(1)} custom-call(bf16[16,256,1024]{2,1,0:T(8,128)(2,1)} %collective-permute-done.5.source), custom_call_target="tpu_custom_call" | custom-call | flops 1677721600 | bytes 16777216 | tf_op jit(solution)/shard_map/pallas_call | solution.py:98
  41.7 1.8 %shard_map.89.before = f32[384,2048]{1,0:T(8,128)S(1)} custom-call(bf16[16,192,128]{2,1,0:T(8,128)(2,1)S(1)} %all-to-all-done.block.firing.a, bf16[16,256,1024]{2,1,0:T(8,128)(2,1)S(1)} %shard_map.87.w, bf16[16,256,1024]{2,1,0:T(8,128)(2,1)S(1)} %shard_map.88.v), custom_call_target="tpu_custom_call" | custom-call | flops 1610612736 | bytes 1048576 | tf_op jit(solution)/shard_map/pallas_call | solution.py:98
  43.5 0.0 collective-permute-done.6.other
  43.5 4.9 %collective-permute-done.2.two.b = bf16[16,192,128]{2,1,0:T(8,128)(2,1)} collective-permute-done((bf16[16,192,128]{2,1,0:T(8,128)(2,1)S(1)}, bf16[16,192,128]{2,1,0:T(8,128)(2,1)}, u32[]{:S(2)}, u32[]{:S(2)}) %collective-permute-start.2) | collective-permute-done | bytes 786464 | tf_op jit(solution)/shard_map/ppermute | solution.py:48
  48.4 0.2 collective-permute-done.3.a
  48.6 0.0 copy-start.1
  48.6 3.0 %collective-permute-done.4.b = bf16[16,192,128]{2,1,0:T(8,128)(2,1)S(1)} collective-permute-done((bf16[16,192,128]{2,1,0:T(8,128)(2,1)S(1)}, bf16[16,192,128]{2,1,0:T(8,128)(2,1)S(1)}, u32[]{:S(2)}, u32[]{:S(2)}) %collective-permute-start.4) | collective-permute-done | bytes 786464 | tf_op jit(solution)/shard_map/ppermute | solution.py:48
  51.6 0.0 copy-start.3
  51.6 7.3 %shard_map.90 = (bf16[384,1024]{1,0:T(8,128)(2,1)S(1)}, bf16[384,1024]{1,0:T(8,128)(2,1)S(1)}, f32[16,128]{1,0:T(8,128)S(1)}) custom-call(bf16[16,192,128]{2,1,0:T(8,128)(2,1)} %collective-permute-done.2.two.b, bf16[16,192,128]{2,1,0:T(8,128)(2,1)S(1)} %collective-permute-done.3.a, bf16[16,192,128]{2,1,0:T(8,128)(2,1)S(1)} %collective-permute-done.4.b, ...), custom_call_target="tpu_custom_call" | custom-call | flops 4831838208 | bytes 1048576 | tf_op jit(solution)/shard_map/pallas_call | solution.py:98
  59.0 0.0 copy-done.1
  59.0 0.0 copy-done.3
  59.0 3.5 %shard_map.92 = (bf16[16,208,128]{2,1,0:T(8,128)(2,1)S(1)}, bf16[16,208,128]{2,1,0:T(8,128)(2,1)S(1)}) custom-call(bf16[384,1024]{1,0:T(8,128)(2,1)S(1)} %get-tuple-element.23.signal, bf16[384,1024]{1,0:T(8,128)(2,1)S(1)} %get-tuple-element.24.signal_other, bf16[16,256,1024]{2,1,0:T(8,128)(2,1)S(1)} %shard_map.87.w, bf16[16,256,1024]{2,1,0:T(8,128)(2,1)S(1)} %shard_map.88.v, ...), custom_call_target="tpu_custom_call" | custom-call | flops 3221225472 | bytes 1048576 | tf_op jit(solution)/shard_map/pallas_call | solution.py:98
  62.5 0.4 collective-permute-start.7
  62.8 3.5 %shard_map.91 = (bf16[16,208,128]{2,1,0:T(8,128)(2,1)S(1)}, bf16[16,208,128]{2,1,0:T(8,128)(2,1)S(1)}) custom-call(bf16[384,1024]{1,0:T(8,128)(2,1)S(1)} %get-tuple-element.23.signal, bf16[384,1024]{1,0:T(8,128)(2,1)S(1)} %get-tuple-element.24.signal_other, bf16[16,256,1024]{2,1,0:T(8,128)(2,1)S(1)} %shard_map.87.w, bf16[16,256,1024]{2,1,0:T(8,128)(2,1)S(1)} %shard_map.88.v, ...), custom_call_target="tpu_custom_call" | custom-call | flops 3221225472 | bytes 1048576 | tf_op jit(solution)/shard_map/pallas_call | solution.py:98
  66.3 0.3 collective-permute-start.8
  66.6 1.2 %collective-permute-start.9 = (bf16[16,208,128]{2,1,0:T(8,128)(2,1)S(1)}, bf16[16,208,128]{2,1,0:T(8,128)(2,1)S(1)}, u32[]{:S(2)}, u32[]{:S(2)}) collective-permute-start(bf16[16,208,128]{2,1,0:T(8,128)(2,1)S(1)} %get-tuple-element.30), channel_id=1, source_target_pairs={{96,0},{25,1},{98,2},{27,3},{100,4},{29,5},{102,6},{31,7},{104,8},... | collective-permute-start | bytes 2555912 | tf_op jit(solution)/shard_map/ppermute | solution.py:48
  67.8 5.0 %collective-permute-start.16 = (bf16[16,192,128]{2,1,0:T(8,128)(2,1)S(1)}, bf16[16,192,128]{2,1,0:T(8,128)(2,1)}, u32[]{:S(2)}, u32[]{:S(2)}) collective-permute-start(bf16[16,192,128]{2,1,0:T(8,128)(2,1)S(1)} %all-to-all-done.block.firing.a), channel_id=1, source_target_pairs={{0,1},{1,0},{2,3},{3,2},{4,5},{5,4},{6,7},{7,6},{8,9},{9,8},{10,11... | collective-permute-start | bytes 2359304 | tf_op jit(solution)/shard_map/ppermute | solution.py:56
  72.8 0.0 collective-permute-start.17
  72.8 1.5 %collective-permute-done.7.one = bf16[16,208,128]{2,1,0:T(8,128)(2,1)S(1)} collective-permute-done((bf16[16,208,128]{2,1,0:T(8,128)(2,1)S(1)}, bf16[16,208,128]{2,1,0:T(8,128)(2,1)S(1)}, u32[]{:S(2)}, u32[]{:S(2)}) %collective-permute-start.7) | collective-permute-done | bytes 852000 | tf_op jit(solution)/shard_map/ppermute | solution.py:48
  74.4 3.0 %collective-permute-start.15 = (bf16[384,1024]{1,0:T(8,128)(2,1)S(1)}, bf16[384,1024]{1,0:T(8,128)(2,1)}, u32[]{:S(2)}, u32[]{:S(2)}) collective-permute-start(bf16[384,1024]{1,0:T(8,128)(2,1)S(1)} %get-tuple-element.24.signal_other), channel_id=1, source_target_pairs={{0,1},{1,0},{2,3},{3,2},{4,5},{5,4},{6,7},{7,6},{8,9},{9,8},{10,11... | collective-permute-start | bytes 2359304 | tf_op jit(solution)/shard_map/ppermute | solution.py:56
  77.4 2.3 %collective-permute-done.8.two = bf16[16,208,128]{2,1,0:T(8,128)(2,1)S(1)} collective-permute-done((bf16[16,208,128]{2,1,0:T(8,128)(2,1)S(1)}, bf16[16,208,128]{2,1,0:T(8,128)(2,1)S(1)}, u32[]{:S(2)}, u32[]{:S(2)}) %collective-permute-start.8) | collective-permute-done | bytes 852000 | tf_op jit(solution)/shard_map/ppermute | solution.py:48
  79.6 0.1 collective-permute-done.9.three
  79.7 1.4 %shard_map.93 = bf16[16,208,128]{2,1,0:T(8,128)(2,1)} custom-call(bf16[16,208,128]{2,1,0:T(8,128)(2,1)S(1)} %get-tuple-element.27.own, bf16[16,208,128]{2,1,0:T(8,128)(2,1)S(1)} %collective-permute-done.7.one, bf16[16,208,128]{2,1,0:T(8,128)(2,1)S(1)} %collective-permute-done.8.two, bf16[16,208,128]{2,1,0:T(8,128)(2,1)S(1)} %collective-permute-done.9.three), custom_call_target="tpu_custom_call" | custom-call | flops 1048576 | bytes 1048576 | tf_op jit(solution)/shard_map/pallas_call | solution.py:98
  81.1 4.7 %all-to-all-start.1 = ((bf16[16,208,128]{2,1,0:T(8,128)(2,1)}), bf16[16,208,128]{2,1,0:T(8,128)(2,1)S(1)}, u32[]{:S(2)}, u32[]{:S(2)}) async-start(bf16[16,208,128]{2,1,0:T(8,128)(2,1)} %shard_map.93), calls=%async_computation.1 | async-start | bytes 1703936 | tf_op jit(solution)/shard_map/all_to_all | solution.py:52
  85.8 5.4 %collective-permute-start.13 = (bf16[16,192,128]{2,1,0:T(8,128)(2,1)}, bf16[16,192,128]{2,1,0:T(8,128)(2,1)}, u32[]{:S(2)}, u32[]{:S(2)}) collective-permute-start(bf16[16,192,128]{2,1,0:T(8,128)(2,1)} %copy-done.1), channel_id=1, source_target_pairs={{0,1},{1,0},{2,3},{3,2},{4,5},{5,4},{6,7},{7,6},{8,9},{9,8},{10,11... | collective-permute-start | bytes 2359304 | tf_op jit(solution)/shard_map/ppermute | solution.py:56
  91.2 0.1 collective-permute-start.14
  91.3 0.0 collective-permute-done.16.a_other
  91.3 0.0 collective-permute-done.17.b_other
  91.3 0.0 collective-permute-done.15.signal_other
  91.3 7.3 %shard_map.96.rest_0_ = bf16[16,256,1024]{2,1,0:T(8,128)(2,1)} custom-call(bf16[16,192,128]{2,1,0:T(8,128)(2,1)S(1)} %all-to-all-done.block.firing.a, bf16[16,192,128]{2,1,0:T(8,128)(2,1)} %collective-permute-done.2.two.b, bf16[16,192,128]{2,1,0:T(8,128)(2,1)} %collective-permute-done.16.a_other, bf16[16,192,128]{2,1,0:T(8,128)(2,1)} %collective-permute-done.17.b_other, ...), custom_call_target="tpu_custom_call" | custom-call | flops 3221225472 | bytes 1048576 | tf_op jit(solution)/shard_map/pallas_call | solution.py:98
  98.7 0.0 all-to-all-done.1.arrived
  98.7 0.3 shard_map.94.own
  98.9 3.2 %collective-permute-start.10 = (bf16[208,128]{1,0:T(8,128)(2,1)S(1)}, bf16[208,128]{1,0:T(8,128)(2,1)S(1)}, u32[]{:S(2)}, u32[]{:S(2)}) collective-permute-start(bf16[208,128]{1,0:T(8,128)(2,1)S(1)} %shard_map.94.own), channel_id=1, source_target_pairs={{0,2},{2,0},{1,3},{3,1},{4,6},{6,4},{5,7},{7,5},{8,10},{10,8},{9,1... | collective-permute-start | bytes 159752 | tf_op jit(solution)/shard_map/ppermute | solution.py:56
  102.1 3.2 %collective-permute-start.11 = (bf16[208,128]{1,0:T(8,128)(2,1)S(1)}, bf16[208,128]{1,0:T(8,128)(2,1)S(1)}, u32[]{:S(2)}, u32[]{:S(2)}) collective-permute-start(bf16[208,128]{1,0:T(8,128)(2,1)S(1)} %shard_map.94.own), channel_id=1, source_target_pairs={{0,1},{1,0},{2,3},{3,2},{4,5},{5,4},{6,7},{7,6},{8,9},{9,8},{10,11... | collective-permute-start | bytes 159752 | tf_op jit(solution)/shard_map/ppermute | solution.py:56
  105.3 0.2 collective-permute-start.12
  105.5 0.0 collective-permute-done.13.a_other
  105.5 0.0 collective-permute-done.14.b_other
  105.6 1.1 copy-done.2
  106.7 1.1 copy-done.4
  107.8 7.1 %shard_map.97 = bf16[16,256,1024]{2,1,0:T(8,128)(2,1)} custom-call(bf16[16,192,128]{2,1,0:T(8,128)(2,1)S(1)} %copy-done.2, bf16[16,192,128]{2,1,0:T(8,128)(2,1)S(1)} %copy-done.4, bf16[16,192,128]{2,1,0:T(8,128)(2,1)} %collective-permute-done.13.a_other, bf16[16,192,128]{2,1,0:T(8,128)(2,1)} %collective-permute-done.14.b_other, ...), custom_call_target="tpu_custom_call", output_to_operand_aliasing={{}: (6, {})} | custom-call | flops 3221225472 | bytes 1048576 | tf_op jit(solution)/shard_map/pallas_call | solution.py:98
  114.9 0.0 collective-permute-done.10.beside
  114.9 0.0 collective-permute-done.11.opposite
  114.9 0.0 collective-permute-done.12.last
  114.9 0.0 copy-done
  115.0 1.4 %shard_map.95 = (bf16[1024,128]{1,0:T(8,128)(2,1)}, f32[1,128]{1,0:T(1,128)}, f32[1,1]{1,0:T(1,128)}) custom-call(bf16[768,1024]{1,0:T(8,128)(2,1)S(1)} %bitcast.9, bf16[208,128]{1,0:T(8,128)(2,1)S(1)} %shard_map.94.own, bf16[208,128]{1,0:T(8,128)(2,1)S(1)} %collective-permute-done.10.beside, bf16[208,128]{1,0:T(8,128)(2,1)S(1)} %collective-permute-done.11.opposite, ...), custom_call_target="tpu_custom_call" | custom-call | flops 1048576 | bytes 1048576 | tf_op jit(solution)/shard_map/pallas_call | solution.py:98
  (5 shorter events, 0.1 us)
Async XLA Ops:
  2.2 2.5 %collective-permute-start = (f32[384,128]{1,0:T(8,128)S(1)}, f32[384,128]{1,0:T(8,128)S(1)}, u32[]{:S(2)}, u32[]{:S(2)}) collective-permute-start(f32[384,128]{1,0:T(8,128)S(1)} %shard_map.85), channel_id=1, source_target_pairs={{0,1},{1,0},{2,3},{3,2},{4,5},{5,4},{6,7},{7,6},{8,9},{9,8},{10,11... | collective-permute-start | bytes 589832 | tf_op jit(solution)/shard_map/ppermute | solution.py:56
  4.8 35.7 %collective-permute-start.5 = (bf16[16,256,1024]{2,1,0:T(8,128)(2,1)}, bf16[16,256,1024]{2,1,0:T(8,128)(2,1)}, u32[]{:S(2)}, u32[]{:S(2)}) collective-permute-start(bf16[16,256,1024]{2,1,0:T(8,128)(2,1)} %bitcast.11), channel_id=1, source_target_pairs={{0,1},{1,0},{2,3},{3,2},{4,5},{5,4},{6,7},{7,6},{8,9},{9,8},{10,11... | collective-permute-start | bytes 25165832 | tf_op jit(solution)/shard_map/ppermute | solution.py:56
  5.1 0.7 copy-start.5
  7.4 4.3 %collective-permute-start.1 = (f32[192,128]{1,0:T(8,128)S(1)}, f32[192,128]{1,0:T(8,128)S(1)}, u32[]{:S(2)}, u32[]{:S(2)}) collective-permute-start(f32[192,128]{1,0:T(8,128)S(1)} %constant_dynamic-slice_fusion.1), channel_id=1, source_target_pairs={{0,2},{2,0},{1,3},{3,1},{4,6},{6,4},{5,7},{7,5},{8,10},{10,8},{9,1... | collective-permute-start | bytes 294920 | tf_op jit(solution)/shard_map/ppermute | solution.py:56
  12.7 24.5 %all-to-all-start = ((bf16[16,192,128]{2,1,0:T(8,128)(2,1)}), bf16[16,192,128]{2,1,0:T(8,128)(2,1)S(1)}, u32[]{:S(2)}, u32[]{:S(2)}) async-start(bf16[16,192,128]{2,1,0:T(8,128)(2,1)} %get-tuple-element.20), calls=%async_computation | async-start | bytes 1572864 | tf_op jit(solution)/shard_map/all_to_all | solution.py:52
  24.1 19.4 %collective-permute-start.6 = (bf16[384,1024]{1,0:T(8,128)(2,1)S(1)}, bf16[384,1024]{1,0:T(8,128)(2,1)S(1)}, u32[]{:S(2)}, u32[]{:S(2)}) collective-permute-start(bf16[384,1024]{1,0:T(8,128)(2,1)S(1)} %constant_dynamic-slice_fusion), channel_id=1, source_target_pairs={{0,1},{1,0},{2,3},{3,2},{4,5},{5,4},{6,7},{7,6},{8,9},{9,8},{10,11... | collective-permute-start | bytes 2359304 | tf_op jit(solution)/shard_map/ppermute | solution.py:56
  37.2 11.2 %collective-permute-start.2 = (bf16[16,192,128]{2,1,0:T(8,128)(2,1)S(1)}, bf16[16,192,128]{2,1,0:T(8,128)(2,1)}, u32[]{:S(2)}, u32[]{:S(2)}) collective-permute-start(bf16[16,192,128]{2,1,0:T(8,128)(2,1)S(1)} %all-to-all-done.block.firing.a), channel_id=1, source_target_pairs={{0,2},{1,7},{2,4},{3,1},{4,6},{5,3},{6,0},{7,5},{8,10},{9,15},{10,... | collective-permute-start | bytes 2359304 | tf_op jit(solution)/shard_map/ppermute | solution.py:48
  37.4 11.2 %collective-permute-start.3 = (bf16[16,192,128]{2,1,0:T(8,128)(2,1)S(1)}, bf16[16,192,128]{2,1,0:T(8,128)(2,1)S(1)}, u32[]{:S(2)}, u32[]{:S(2)}) collective-permute-start(bf16[16,192,128]{2,1,0:T(8,128)(2,1)S(1)} %all-to-all-done.block.firing.a), channel_id=1, source_target_pairs={{0,96},{1,25},{2,98},{3,27},{4,100},{5,29},{6,102},{7,31},{8,104},... | collective-permute-start | bytes 2359304 | tf_op jit(solution)/shard_map/ppermute | solution.py:48
  39.2 12.5 %collective-permute-start.4 = (bf16[16,192,128]{2,1,0:T(8,128)(2,1)S(1)}, bf16[16,192,128]{2,1,0:T(8,128)(2,1)S(1)}, u32[]{:S(2)}, u32[]{:S(2)}) collective-permute-start(bf16[16,192,128]{2,1,0:T(8,128)(2,1)S(1)} %all-to-all-done.block.firing.a), channel_id=1, source_target_pairs={{0,32},{1,9},{2,34},{3,11},{4,36},{5,13},{6,38},{7,15},{8,40},{9,1... | collective-permute-start | bytes 2359304 | tf_op jit(solution)/shard_map/ppermute | solution.py:48
  48.6 10.4 %copy-start.1 = (bf16[16,192,128]{2,1,0:T(8,128)(2,1)}, bf16[16,192,128]{2,1,0:T(8,128)(2,1)S(1)}, u32[]{:S(2)}) copy-start(bf16[16,192,128]{2,1,0:T(8,128)(2,1)S(1)} %collective-permute-done.3.a) | copy-start | bytes 2359300
  51.6 7.4 %copy-start.3 = (bf16[16,192,128]{2,1,0:T(8,128)(2,1)}, bf16[16,192,128]{2,1,0:T(8,128)(2,1)S(1)}, u32[]{:S(2)}) copy-start(bf16[16,192,128]{2,1,0:T(8,128)(2,1)S(1)} %collective-permute-done.4.b) | copy-start | bytes 2359300
  62.5 11.9 %collective-permute-start.7 = (bf16[16,208,128]{2,1,0:T(8,128)(2,1)S(1)}, bf16[16,208,128]{2,1,0:T(8,128)(2,1)S(1)}, u32[]{:S(2)}, u32[]{:S(2)}) collective-permute-start(bf16[16,208,128]{2,1,0:T(8,128)(2,1)S(1)} %get-tuple-element.28), channel_id=1, source_target_pairs={{32,0},{9,1},{34,2},{11,3},{36,4},{13,5},{38,6},{15,7},{40,8},{17,... | collective-permute-start | bytes 2555912 | tf_op jit(solution)/shard_map/ppermute | solution.py:48
  66.3 13.3 %collective-permute-start.8 = (bf16[16,208,128]{2,1,0:T(8,128)(2,1)S(1)}, bf16[16,208,128]{2,1,0:T(8,128)(2,1)S(1)}, u32[]{:S(2)}, u32[]{:S(2)}) collective-permute-start(bf16[16,208,128]{2,1,0:T(8,128)(2,1)S(1)} %get-tuple-element.29), channel_id=1, source_target_pairs={{2,0},{7,1},{4,2},{1,3},{6,4},{3,5},{0,6},{5,7},{10,8},{15,9},{12,... | collective-permute-start | bytes 2555912 | tf_op jit(solution)/shard_map/ppermute | solution.py:48
  66.6 13.1 %collective-permute-start.9 = (bf16[16,208,128]{2,1,0:T(8,128)(2,1)S(1)}, bf16[16,208,128]{2,1,0:T(8,128)(2,1)S(1)}, u32[]{:S(2)}, u32[]{:S(2)}) collective-permute-start(bf16[16,208,128]{2,1,0:T(8,128)(2,1)S(1)} %get-tuple-element.30), channel_id=1, source_target_pairs={{96,0},{25,1},{98,2},{27,3},{100,4},{29,5},{102,6},{31,7},{104,8},... | collective-permute-start | bytes 2555912 | tf_op jit(solution)/shard_map/ppermute | solution.py:48
  67.8 23.5 %collective-permute-start.16 = (bf16[16,192,128]{2,1,0:T(8,128)(2,1)S(1)}, bf16[16,192,128]{2,1,0:T(8,128)(2,1)}, u32[]{:S(2)}, u32[]{:S(2)}) collective-permute-start(bf16[16,192,128]{2,1,0:T(8,128)(2,1)S(1)} %all-to-all-done.block.firing.a), channel_id=1, source_target_pairs={{0,1},{1,0},{2,3},{3,2},{4,5},{5,4},{6,7},{7,6},{8,9},{9,8},{10,11... | collective-permute-start | bytes 2359304 | tf_op jit(solution)/shard_map/ppermute | solution.py:56
  72.8 18.5 %collective-permute-start.17 = (bf16[16,192,128]{2,1,0:T(8,128)(2,1)}, bf16[16,192,128]{2,1,0:T(8,128)(2,1)}, u32[]{:S(2)}, u32[]{:S(2)}) collective-permute-start(bf16[16,192,128]{2,1,0:T(8,128)(2,1)} %collective-permute-done.2.two.b), channel_id=1, source_target_pairs={{0,1},{1,0},{2,3},{3,2},{4,5},{5,4},{6,7},{7,6},{8,9},{9,8},{10,11... | collective-permute-start | bytes 2359304 | tf_op jit(solution)/shard_map/ppermute | solution.py:56
  74.4 16.9 %collective-permute-start.15 = (bf16[384,1024]{1,0:T(8,128)(2,1)S(1)}, bf16[384,1024]{1,0:T(8,128)(2,1)}, u32[]{:S(2)}, u32[]{:S(2)}) collective-permute-start(bf16[384,1024]{1,0:T(8,128)(2,1)S(1)} %get-tuple-element.24.signal_other), channel_id=1, source_target_pairs={{0,1},{1,0},{2,3},{3,2},{4,5},{5,4},{6,7},{7,6},{8,9},{9,8},{10,11... | collective-permute-start | bytes 2359304 | tf_op jit(solution)/shard_map/ppermute | solution.py:56
  81.1 17.6 %all-to-all-start.1 = ((bf16[16,208,128]{2,1,0:T(8,128)(2,1)}), bf16[16,208,128]{2,1,0:T(8,128)(2,1)S(1)}, u32[]{:S(2)}, u32[]{:S(2)}) async-start(bf16[16,208,128]{2,1,0:T(8,128)(2,1)} %shard_map.93), calls=%async_computation.1 | async-start | bytes 1703936 | tf_op jit(solution)/shard_map/all_to_all | solution.py:52
  85.8 19.7 %collective-permute-start.13 = (bf16[16,192,128]{2,1,0:T(8,128)(2,1)}, bf16[16,192,128]{2,1,0:T(8,128)(2,1)}, u32[]{:S(2)}, u32[]{:S(2)}) collective-permute-start(bf16[16,192,128]{2,1,0:T(8,128)(2,1)} %copy-done.1), channel_id=1, source_target_pairs={{0,1},{1,0},{2,3},{3,2},{4,5},{5,4},{6,7},{7,6},{8,9},{9,8},{10,11... | collective-permute-start | bytes 2359304 | tf_op jit(solution)/shard_map/ppermute | solution.py:56
  91.2 14.3 %collective-permute-start.14 = (bf16[16,192,128]{2,1,0:T(8,128)(2,1)}, bf16[16,192,128]{2,1,0:T(8,128)(2,1)}, u32[]{:S(2)}, u32[]{:S(2)}) collective-permute-start(bf16[16,192,128]{2,1,0:T(8,128)(2,1)} %copy-done.3), channel_id=1, source_target_pairs={{0,1},{1,0},{2,3},{3,2},{4,5},{5,4},{6,7},{7,6},{8,9},{9,8},{10,11... | collective-permute-start | bytes 2359304 | tf_op jit(solution)/shard_map/ppermute | solution.py:56
  98.9 16.0 %copy-start = (bf16[1,768,1024]{2,1,0:T(8,128)(2,1)S(1)}, bf16[1,768,1024]{2,1,0:T(8,128)(2,1)}, u32[]{:S(2)}) copy-start(bf16[1,768,1024]{2,1,0:T(8,128)(2,1)} %param.5) | copy-start | bytes 4718596
  98.9 16.0 %collective-permute-start.10 = (bf16[208,128]{1,0:T(8,128)(2,1)S(1)}, bf16[208,128]{1,0:T(8,128)(2,1)S(1)}, u32[]{:S(2)}, u32[]{:S(2)}) collective-permute-start(bf16[208,128]{1,0:T(8,128)(2,1)S(1)} %shard_map.94.own), channel_id=1, source_target_pairs={{0,2},{2,0},{1,3},{3,1},{4,6},{6,4},{5,7},{7,5},{8,10},{10,8},{9,1... | collective-permute-start | bytes 159752 | tf_op jit(solution)/shard_map/ppermute | solution.py:56
  102.1 12.8 %collective-permute-start.11 = (bf16[208,128]{1,0:T(8,128)(2,1)S(1)}, bf16[208,128]{1,0:T(8,128)(2,1)S(1)}, u32[]{:S(2)}, u32[]{:S(2)}) collective-permute-start(bf16[208,128]{1,0:T(8,128)(2,1)S(1)} %shard_map.94.own), channel_id=1, source_target_pairs={{0,1},{1,0},{2,3},{3,2},{4,5},{5,4},{6,7},{7,6},{8,9},{9,8},{10,11... | collective-permute-start | bytes 159752 | tf_op jit(solution)/shard_map/ppermute | solution.py:56
  105.3 9.6 %collective-permute-start.12 = (bf16[208,128]{1,0:T(8,128)(2,1)S(1)}, bf16[208,128]{1,0:T(8,128)(2,1)S(1)}, u32[]{:S(2)}, u32[]{:S(2)}) collective-permute-start(bf16[208,128]{1,0:T(8,128)(2,1)S(1)} %shard_map.94.own), channel_id=1, source_target_pairs={{0,3},{1,2},{2,1},{3,0},{4,7},{5,6},{6,5},{7,4},{8,11},{9,10},{10,... | collective-permute-start | bytes 159752 | tf_op jit(solution)/shard_map/ppermute | solution.py:568
  105.5 1.1 copy-start.2
  106.7 1.1 copy-start.4

commit v2 on v1

--- a/solution.py
+++ b/solution.py
@@ -369,7 +369,9 @@
     out = jax.ShapeDtypeStruct((RING * RING, 2 * latent, columns), bf16)
     flops = 2 * 2 * half * columns * 16 * latent
     kernel = functools.partial(gradient_kernel, offset)
-    return call(kernel, args, specs, out, FAR, scratch, flops, 1 << 20, mib=20, input_output_aliases=aliases)
+    return call(
+        kernel, args, specs, out, FAR, scratch, flops, 1 << 20, mib=20, input_output_aliases=aliases
+    )
 
 
 def sum_kernel(own, one, two, three, out):
@@ -390,20 +392,22 @@
 
 def summed(*parts):
     args = [near(part) for part in parts]
-    out = jax.ShapeDtypeStruct(parts[0].shape, bf16)
+    out = near_out(parts[0].shape, bf16)
     return call(sum_kernel, args, [CHIP] * 4, out, CHIP, (), 1 << 20, 1 << 20, mib=4)
 
 
 def encode_kernel(flip, inputs, weights, *rest):
     place = placement()
-    out, rows_here, weights_here, sems = rest[-4:]
+    out, rows_here, weights_here, bias_here, sems = rest[-5:]
     half = out.shape[0]
     which = 1 - place[2] if flip else place[2]
     rows = pl.ds(pl.multiple_of(which * half, 16), half)
-    copies = (
+    copies = [
         pltpu.make_async_copy(inputs.at[rows, :], rows_here, sems.at[0]),
         pltpu.make_async_copy(weights, weights_here, sems.at[1]),
-    )
+    ]
+    if not flip:
+        copies.append(pltpu.make_async_copy(rest[0], bias_here, sems.at[2]))
     for copy in copies:
         copy.start()
     for copy in copies:
@@ -413,7 +417,7 @@
 
         @pl.when(place[3] == 0)
         def _():
-            out[...] += rest[0][...]
+            out[...] += bias_here[...]
 
 
 def encoded(flip, inputs, weights, bias):
@@ -422,12 +426,13 @@
     scratch = [
         pltpu.VMEM((tokens // 2, columns), bf16),
         pltpu.VMEM((columns, latent), bf16),
-        pltpu.SemaphoreType.DMA((2,)),
+        pltpu.VMEM((1, latent), f32),
+        pltpu.SemaphoreType.DMA((3,)),
     ]
     out = near_out((tokens // 2, latent), f32)
     kernel = functools.partial(encode_kernel, flip)
-    args = [far(inputs), far(weights)] + ([] if flip else [bias])
-    return call(kernel, args, [FAR, FAR, CHIP][: len(args)], out, CHIP, scratch, 1 << 20, 1 << 20, mib=4)
+    args = [far(inputs), far(weights)] + ([] if flip else [far(bias)])
+    return call(kernel, args, [FAR] * len(args), out, CHIP, scratch, 1 << 20, 1 << 20, mib=4)
 
 
 def fire_kernel(mine, heard, fired, blocks):
@@ -465,8 +470,9 @@
     for tile in range(arrived.shape[0]):
         notes = arrived[tile, quarter:, :].astype(f32)
         losses += [notes[2 * i : 2 * i + 1] + notes[2 * i + 1 : 2 * i + 2] for i in range(RING)]
-    unit = jnp.maximum(functools.reduce(jnp.maximum, losses), 1e-30)
-    whole = functools.reduce(lambda p, q: p + q, [jnp.round(value / unit * 65536.0) for value in losses])
+    losses = jnp.concatenate(losses, axis=0)
+    unit = jnp.maximum(jnp.max(losses, axis=0, keepdims=True), 1e-30)
+    whole = jnp.sum(jnp.round(losses * (65536.0 / unit)), axis=0, keepdims=True)
     loss = jnp.broadcast_to(whole * (unit / 65536.0), (8, latent))
     high = loss.astype(bf16).astype(f32)
     delta[quarter:, :] = jnp.concatenate([high, loss - high], axis=0).astype(bf16)
@@ -509,7 +515,9 @@
     )
     scratch = [pltpu.VMEM((tokens, latent), bf16)]
     kernel = functools.partial(finish_kernel, size)
-    return call(kernel, args, [CHIP] * 5, outs, (CHIP, CHIP, SCALARS), scratch, 1 << 20, 1 << 20, mib=8)
+    return call(
+        kernel, args, [CHIP] * 5, outs, (CHIP, CHIP, SCALARS), scratch, 1 << 20, 1 << 20, mib=8
+    )
 
 
 def whole_step(mlp_inputs, mlp_outputs, encoders, encoder_bias, decoders):

time: 117 us -> 117 us (level)
    unnamed x12 -> x10, local copies, waits for them, and re-layouts: 2.93 us -> 2.28 us
where the time goes in v2:
time: 117 us; the launch traced here: 116 us
  starting transfers between devices  43.5 us (37%)
  Pallas kernels  40.1 us (34%)
  waiting for transfers between devices  27.6 us (24%)
  local copies, waits for them, and re-layouts  3.48 us (3%)
    pallas_call x14, Pallas kernels, call(): pl.pallas_call(kernel, in_specs=specs, out_specs=out_specs, out_shape=out...  40.1 us
    ppermute x11, starting transfers between devices, swapped(): return lax.ppermute(array, axis, SWAP)  24.6 us
    all_to_all x2, starting transfers between devices, in_coset(): lax.all_to_all(blocks, AXES, 0, 0, axis_index_groups=COSETS, tiled=True)  14.9 us
    ppermute x6, waiting for transfers between devices, sent(): return lax.ppermute(array, AXES, toward(shift, back))  12 us
    all_to_all x2, waiting for transfers between devices, in_coset(): lax.all_to_all(blocks, AXES, 0, 0, axis_index_groups=COSETS, tiled=True)  11.8 us
    ppermute x11, waiting for transfers between devices, swapped(): return lax.ppermute(array, axis, SWAP)  3.91 us
    ppermute x6, starting transfers between devices, sent(): return lax.ppermute(array, AXES, toward(shift, back))  3.87 us
  transfers between devices with their start and end apart: 20, of which 9 were waited for; matrix products, arithmetic and copies ran while one was open for 1% of the time, Pallas kernels for 23%

profile of v2, /device:TPU:1, one launch (start us, length us, event | category | flops | bytes accessed | tf_op | source)
XLA Modules:
  0.0 115.8 jit_solution(17128584278116391188)
XLA Ops:
  0.6 1.6 %shard_map.85 = f32[384,128]{1,0:T(8,128)S(1)} custom-call(bf16[768,1024]{1,0:T(8,128)(2,1)} %bitcast.7, bf16[1024,128]{1,0:T(8,128)(2,1)} %bitcast.15), custom_call_target="tpu_custom_call" | custom-call | flops 1048576 | bytes 1048576 | tf_op jit(solution)/shard_map/pallas_call | solution.py:98
  2.2 1.5 %collective-permute-start = (f32[384,128]{1,0:T(8,128)S(1)}, f32[384,128]{1,0:T(8,128)S(1)}, u32[]{:S(2)}, u32[]{:S(2)}) collective-permute-start(f32[384,128]{1,0:T(8,128)S(1)} %shard_map.85), channel_id=1, source_target_pairs={{0,1},{1,0},{2,3},{3,2},{4,5},{5,4},{6,7},{7,6},{8,9},{9,8},{10,11... | collective-permute-start | bytes 589832 | tf_op jit(solution)/shard_map/ppermute | solution.py:56
  3.7 1.1 collective-permute-done
  4.8 0.4 collective-permute-start.5
  5.1 1.6 %shard_map.84 = f32[384,128]{1,0:T(8,128)S(1)} custom-call(bf16[768,1024]{1,0:T(8,128)(2,1)} %bitcast.8, bf16[1024,128]{1,0:T(8,128)(2,1)} %bitcast.16, f32[1,128]{1,0:T(1,128)} %rest_0_.1), custom_call_target="tpu_custom_call" | custom-call | flops 1048576 | bytes 1048576 | tf_op jit(solution)/shard_map/pallas_call | solution.py:98
  6.8 1.5 %collective-permute-start.1 = (f32[192,128]{1,0:T(8,128)S(1)}, f32[192,128]{1,0:T(8,128)S(1)}, u32[]{:S(2)}, u32[]{:S(2)}) collective-permute-start(f32[192,128]{1,0:T(8,128)S(1)} %constant_dynamic-slice_fusion.1), channel_id=1, source_target_pairs={{0,2},{2,0},{1,3},{3,1},{4,6},{6,4},{5,7},{7,5},{8,10},{10,8},{9,1... | collective-permute-start | bytes 294920 | tf_op jit(solution)/shard_map/ppermute | solution.py:56
  8.3 2.8 %collective-permute-done.1.heard = f32[192,128]{1,0:T(8,128)S(1)} collective-permute-done((f32[192,128]{1,0:T(8,128)S(1)}, f32[192,128]{1,0:T(8,128)S(1)}, u32[]{:S(2)}, u32[]{:S(2)}) %collective-permute-start.1) | collective-permute-done | bytes 98336 | tf_op jit(solution)/shard_map/ppermute | solution.py:56
  11.1 1.0 shard_map.86
  12.1 10.2 %all-to-all-start = ((bf16[16,192,128]{2,1,0:T(8,128)(2,1)}), bf16[16,192,128]{2,1,0:T(8,128)(2,1)S(1)}, u32[]{:S(2)}, u32[]{:S(2)}) async-start(bf16[16,192,128]{2,1,0:T(8,128)(2,1)} %get-tuple-element.20), calls=%async_computation | async-start | bytes 1572864 | tf_op jit(solution)/shard_map/all_to_all | solution.py:52
  22.2 1.2 %constant_dynamic-slice_fusion = bf16[384,1024]{1,0:T(8,128)(2,1)S(1)} fusion(bf16[768,1024]{1,0:T(8,128)(2,1)} %bitcast.13, s32[]{:T(128)S(6)} %select_n.7), kind=kLoop, calls=%fused_computation | loop fusion | bytes 1572868 | tf_op jit(solution)/shard_map/dynamic_slice | solution.py:541
  23.4 1.4 %collective-permute-start.6 = (bf16[384,1024]{1,0:T(8,128)(2,1)S(1)}, bf16[384,1024]{1,0:T(8,128)(2,1)S(1)}, u32[]{:S(2)}, u32[]{:S(2)}) collective-permute-start(bf16[384,1024]{1,0:T(8,128)(2,1)S(1)} %constant_dynamic-slice_fusion), channel_id=1, source_target_pairs={{0,1},{1,0},{2,3},{3,2},{4,5},{5,4},{6,7},{7,6},{8,9},{9,8},{10,11... | collective-permute-start | bytes 2359304 | tf_op jit(solution)/shard_map/ppermute | solution.py:56
  24.8 11.8 %all-to-all-done.block.firing.a = bf16[16,192,128]{2,1,0:T(8,128)(2,1)S(1)} async-done(((bf16[16,192,128]{2,1,0:T(8,128)(2,1)}), bf16[16,192,128]{2,1,0:T(8,128)(2,1)S(1)}, u32[]{:S(2)}, u32[]{:S(2)}) %all-to-all-start) | async-done | bytes 786464 | tf_op jit(solution)/shard_map/all_to_all | solution.py:52
  36.6 0.2 collective-permute-start.2
  36.7 1.8 %collective-permute-start.3 = (bf16[16,192,128]{2,1,0:T(8,128)(2,1)S(1)}, bf16[16,192,128]{2,1,0:T(8,128)(2,1)S(1)}, u32[]{:S(2)}, u32[]{:S(2)}) collective-permute-start(bf16[16,192,128]{2,1,0:T(8,128)(2,1)S(1)} %all-to-all-done.block.firing.a), channel_id=1, source_target_pairs={{0,96},{1,25},{2,98},{3,27},{4,100},{5,29},{6,102},{7,31},{8,104},... | collective-permute-start | bytes 2359304 | tf_op jit(solution)/shard_map/ppermute | solution.py:48
  38.5 0.0 collective-permute-start.4
  38.5 1.2 %shard_map.87.w = bf16[16,256,1024]{2,1,0:T(8,128)(2,1)S(1)} custom-call(bf16[16,256,1024]{2,1,0:T(8,128)(2,1)} %bitcast.12), custom_call_target="tpu_custom_call" | custom-call | flops 1677721600 | bytes 16777216 | tf_op jit(solution)/shard_map/pallas_call | solution.py:98
  39.8 0.0 collective-permute-done.5.source
  39.8 1.3 %shard_map.88.v = bf16[16,256,1024]{2,1,0:T(8,128)(2,1)S(1)} custom-call(bf16[16,256,1024]{2,1,0:T(8,128)(2,1)} %collective-permute-done.5.source), custom_call_target="tpu_custom_call" | custom-call | flops 1677721600 | bytes 16777216 | tf_op jit(solution)/shard_map/pallas_call | solution.py:98
  41.0 1.8 %shard_map.89.before = f32[384,2048]{1,0:T(8,128)S(1)} custom-call(bf16[16,192,128]{2,1,0:T(8,128)(2,1)S(1)} %all-to-all-done.block.firing.a, bf16[16,256,1024]{2,1,0:T(8,128)(2,1)S(1)} %shard_map.87.w, bf16[16,256,1024]{2,1,0:T(8,128)(2,1)S(1)} %shard_map.88.v), custom_call_target="tpu_custom_call" | custom-call | flops 1610612736 | bytes 1048576 | tf_op jit(solution)/shard_map/pallas_call | solution.py:98
  42.9 0.0 collective-permute-done.6.other
  42.9 4.9 %collective-permute-done.2.two.b = bf16[16,192,128]{2,1,0:T(8,128)(2,1)} collective-permute-done((bf16[16,192,128]{2,1,0:T(8,128)(2,1)S(1)}, bf16[16,192,128]{2,1,0:T(8,128)(2,1)}, u32[]{:S(2)}, u32[]{:S(2)}) %collective-permute-start.2) | collective-permute-done | bytes 786464 | tf_op jit(solution)/shard_map/ppermute | solution.py:48
  47.8 0.2 collective-permute-done.3.a
  48.0 0.0 copy-start.1
  48.0 3.0 %collective-permute-done.4.b = bf16[16,192,128]{2,1,0:T(8,128)(2,1)S(1)} collective-permute-done((bf16[16,192,128]{2,1,0:T(8,128)(2,1)S(1)}, bf16[16,192,128]{2,1,0:T(8,128)(2,1)S(1)}, u32[]{:S(2)}, u32[]{:S(2)}) %collective-permute-start.4) | collective-permute-done | bytes 786464 | tf_op jit(solution)/shard_map/ppermute | solution.py:48
  51.0 0.0 copy-start.3
  51.0 7.3 %shard_map.90 = (bf16[384,1024]{1,0:T(8,128)(2,1)S(1)}, bf16[384,1024]{1,0:T(8,128)(2,1)S(1)}, f32[16,128]{1,0:T(8,128)S(1)}) custom-call(bf16[16,192,128]{2,1,0:T(8,128)(2,1)} %collective-permute-done.2.two.b, bf16[16,192,128]{2,1,0:T(8,128)(2,1)S(1)} %collective-permute-done.3.a, bf16[16,192,128]{2,1,0:T(8,128)(2,1)S(1)} %collective-permute-done.4.b, ...), custom_call_target="tpu_custom_call" | custom-call | flops 4831838208 | bytes 1048576 | tf_op jit(solution)/shard_map/pallas_call | solution.py:98
  58.3 0.0 copy-done.1
  58.3 0.0 copy-done.3
  58.3 3.5 %shard_map.92 = (bf16[16,208,128]{2,1,0:T(8,128)(2,1)S(1)}, bf16[16,208,128]{2,1,0:T(8,128)(2,1)S(1)}) custom-call(bf16[384,1024]{1,0:T(8,128)(2,1)S(1)} %get-tuple-element.23.signal, bf16[384,1024]{1,0:T(8,128)(2,1)S(1)} %get-tuple-element.24.signal_other, bf16[16,256,1024]{2,1,0:T(8,128)(2,1)S(1)} %shard_map.87.w, bf16[16,256,1024]{2,1,0:T(8,128)(2,1)S(1)} %shard_map.88.v, ...), custom_call_target="tpu_custom_call" | custom-call | flops 3221225472 | bytes 1048576 | tf_op jit(solution)/shard_map/pallas_call | solution.py:98
  61.8 0.4 collective-permute-start.7
  62.2 3.5 %shard_map.91 = (bf16[16,208,128]{2,1,0:T(8,128)(2,1)S(1)}, bf16[16,208,128]{2,1,0:T(8,128)(2,1)S(1)}) custom-call(bf16[384,1024]{1,0:T(8,128)(2,1)S(1)} %get-tuple-element.23.signal, bf16[384,1024]{1,0:T(8,128)(2,1)S(1)} %get-tuple-element.24.signal_other, bf16[16,256,1024]{2,1,0:T(8,128)(2,1)S(1)} %shard_map.87.w, bf16[16,256,1024]{2,1,0:T(8,128)(2,1)S(1)} %shard_map.88.v, ...), custom_call_target="tpu_custom_call" | custom-call | flops 3221225472 | bytes 1048576 | tf_op jit(solution)/shard_map/pallas_call | solution.py:98
  65.7 0.3 collective-permute-start.8
  66.0 1.2 %collective-permute-start.9 = (bf16[16,208,128]{2,1,0:T(8,128)(2,1)S(1)}, bf16[16,208,128]{2,1,0:T(8,128)(2,1)S(1)}, u32[]{:S(2)}, u32[]{:S(2)}) collective-permute-start(bf16[16,208,128]{2,1,0:T(8,128)(2,1)S(1)} %get-tuple-element.30), channel_id=1, source_target_pairs={{96,0},{25,1},{98,2},{27,3},{100,4},{29,5},{102,6},{31,7},{104,8},... | collective-permute-start | bytes 2555912 | tf_op jit(solution)/shard_map/ppermute | solution.py:48
  67.2 5.0 %collective-permute-start.16 = (bf16[16,192,128]{2,1,0:T(8,128)(2,1)S(1)}, bf16[16,192,128]{2,1,0:T(8,128)(2,1)}, u32[]{:S(2)}, u32[]{:S(2)}) collective-permute-start(bf16[16,192,128]{2,1,0:T(8,128)(2,1)S(1)} %all-to-all-done.block.firing.a), channel_id=1, source_target_pairs={{0,1},{1,0},{2,3},{3,2},{4,5},{5,4},{6,7},{7,6},{8,9},{9,8},{10,11... | collective-permute-start | bytes 2359304 | tf_op jit(solution)/shard_map/ppermute | solution.py:56
  72.2 0.0 collective-permute-start.17
  72.2 1.5 %collective-permute-done.7.one = bf16[16,208,128]{2,1,0:T(8,128)(2,1)S(1)} collective-permute-done((bf16[16,208,128]{2,1,0:T(8,128)(2,1)S(1)}, bf16[16,208,128]{2,1,0:T(8,128)(2,1)S(1)}, u32[]{:S(2)}, u32[]{:S(2)}) %collective-permute-start.7) | collective-permute-done | bytes 852000 | tf_op jit(solution)/shard_map/ppermute | solution.py:48
  73.7 3.0 %collective-permute-start.15 = (bf16[384,1024]{1,0:T(8,128)(2,1)S(1)}, bf16[384,1024]{1,0:T(8,128)(2,1)}, u32[]{:S(2)}, u32[]{:S(2)}) collective-permute-start(bf16[384,1024]{1,0:T(8,128)(2,1)S(1)} %get-tuple-element.24.signal_other), channel_id=1, source_target_pairs={{0,1},{1,0},{2,3},{3,2},{4,5},{5,4},{6,7},{7,6},{8,9},{9,8},{10,11... | collective-permute-start | bytes 2359304 | tf_op jit(solution)/shard_map/ppermute | solution.py:56
  76.7 2.3 %collective-permute-done.8.two = bf16[16,208,128]{2,1,0:T(8,128)(2,1)S(1)} collective-permute-done((bf16[16,208,128]{2,1,0:T(8,128)(2,1)S(1)}, bf16[16,208,128]{2,1,0:T(8,128)(2,1)S(1)}, u32[]{:S(2)}, u32[]{:S(2)}) %collective-permute-start.8) | collective-permute-done | bytes 852000 | tf_op jit(solution)/shard_map/ppermute | solution.py:48
  79.0 0.1 collective-permute-done.9.three
  79.1 1.4 %shard_map.93 = bf16[16,208,128]{2,1,0:T(8,128)(2,1)} custom-call(bf16[16,208,128]{2,1,0:T(8,128)(2,1)S(1)} %get-tuple-element.27.own, bf16[16,208,128]{2,1,0:T(8,128)(2,1)S(1)} %collective-permute-done.7.one, bf16[16,208,128]{2,1,0:T(8,128)(2,1)S(1)} %collective-permute-done.8.two, bf16[16,208,128]{2,1,0:T(8,128)(2,1)S(1)} %collective-permute-done.9.three), custom_call_target="tpu_custom_call" | custom-call | flops 1048576 | bytes 1048576 | tf_op jit(solution)/shard_map/pallas_call | solution.py:98
  80.5 4.7 %all-to-all-start.1 = ((bf16[16,208,128]{2,1,0:T(8,128)(2,1)}), bf16[16,208,128]{2,1,0:T(8,128)(2,1)S(1)}, u32[]{:S(2)}, u32[]{:S(2)}) async-start(bf16[16,208,128]{2,1,0:T(8,128)(2,1)} %shard_map.93), calls=%async_computation.1 | async-start | bytes 1703936 | tf_op jit(solution)/shard_map/all_to_all | solution.py:52
  85.2 5.4 %collective-permute-start.13 = (bf16[16,192,128]{2,1,0:T(8,128)(2,1)}, bf16[16,192,128]{2,1,0:T(8,128)(2,1)}, u32[]{:S(2)}, u32[]{:S(2)}) collective-permute-start(bf16[16,192,128]{2,1,0:T(8,128)(2,1)} %copy-done.1), channel_id=1, source_target_pairs={{0,1},{1,0},{2,3},{3,2},{4,5},{5,4},{6,7},{7,6},{8,9},{9,8},{10,11... | collective-permute-start | bytes 2359304 | tf_op jit(solution)/shard_map/ppermute | solution.py:56
  90.6 0.1 collective-permute-start.14
  90.7 0.0 collective-permute-done.16.a_other
  90.7 0.0 collective-permute-done.17.b_other
  90.7 0.0 collective-permute-done.15.signal_other
  90.7 7.3 %shard_map.96.rest_0_ = bf16[16,256,1024]{2,1,0:T(8,128)(2,1)} custom-call(bf16[16,192,128]{2,1,0:T(8,128)(2,1)S(1)} %all-to-all-done.block.firing.a, bf16[16,192,128]{2,1,0:T(8,128)(2,1)} %collective-permute-done.2.two.b, bf16[16,192,128]{2,1,0:T(8,128)(2,1)} %collective-permute-done.16.a_other, bf16[16,192,128]{2,1,0:T(8,128)(2,1)} %collective-permute-done.17.b_other, ...), custom_call_target="tpu_custom_call" | custom-call | flops 3221225472 | bytes 1048576 | tf_op jit(solution)/shard_map/pallas_call | solution.py:98
  98.0 0.0 all-to-all-done.1.arrived
  98.0 0.2 shard_map.94.own
  98.2 0.0 copy-start
  98.2 3.2 %collective-permute-start.10 = (bf16[208,128]{1,0:T(8,128)(2,1)S(1)}, bf16[208,128]{1,0:T(8,128)(2,1)S(1)}, u32[]{:S(2)}, u32[]{:S(2)}) collective-permute-start(bf16[208,128]{1,0:T(8,128)(2,1)S(1)} %shard_map.94.own), channel_id=1, source_target_pairs={{0,2},{2,0},{1,3},{3,1},{4,6},{6,4},{5,7},{7,5},{8,10},{10,8},{9,1... | collective-permute-start | bytes 159752 | tf_op jit(solution)/shard_map/ppermute | solution.py:56
  101.4 3.2 %collective-permute-start.11 = (bf16[208,128]{1,0:T(8,128)(2,1)S(1)}, bf16[208,128]{1,0:T(8,128)(2,1)S(1)}, u32[]{:S(2)}, u32[]{:S(2)}) collective-permute-start(bf16[208,128]{1,0:T(8,128)(2,1)S(1)} %shard_map.94.own), channel_id=1, source_target_pairs={{0,1},{1,0},{2,3},{3,2},{4,5},{5,4},{6,7},{7,6},{8,9},{9,8},{10,11... | collective-permute-start | bytes 159752 | tf_op jit(solution)/shard_map/ppermute | solution.py:56
  104.6 0.2 collective-permute-start.12
  104.8 0.0 collective-permute-done.13.a_other
  104.8 0.0 collective-permute-done.14.b_other
  104.8 0.0 copy-start.2
  104.8 1.1 copy-done.2
  106.0 1.1 copy-done.4
  107.1 7.1 %shard_map.97 = bf16[16,256,1024]{2,1,0:T(8,128)(2,1)} custom-call(bf16[16,192,128]{2,1,0:T(8,128)(2,1)S(1)} %copy-done.2, bf16[16,192,128]{2,1,0:T(8,128)(2,1)S(1)} %copy-done.4, bf16[16,192,128]{2,1,0:T(8,128)(2,1)} %collective-permute-done.13.a_other, bf16[16,192,128]{2,1,0:T(8,128)(2,1)} %collective-permute-done.14.b_other, ...), custom_call_target="tpu_custom_call", output_to_operand_aliasing={{}: (6, {})} | custom-call | flops 3221225472 | bytes 1048576 | tf_op jit(solution)/shard_map/pallas_call | solution.py:98
  114.2 0.0 collective-permute-done.10.beside
  114.2 0.0 collective-permute-done.11.opposite
  114.2 0.0 collective-permute-done.12.last
  114.2 0.0 copy-done
  114.2 1.4 %shard_map.95 = (bf16[1024,128]{1,0:T(8,128)(2,1)}, f32[1,128]{1,0:T(1,128)}, f32[1,1]{1,0:T(1,128)}) custom-call(bf16[768,1024]{1,0:T(8,128)(2,1)S(1)} %bitcast.9, bf16[208,128]{1,0:T(8,128)(2,1)S(1)} %shard_map.94.own, bf16[208,128]{1,0:T(8,128)(2,1)S(1)} %collective-permute-done.10.beside, bf16[208,128]{1,0:T(8,128)(2,1)S(1)} %collective-permute-done.11.opposite, ...), custom_call_target="tpu_custom_call" | custom-call | flops 1048576 | bytes 1048576 | tf_op jit(solution)/shard_map/pallas_call | solution.py:98
  (3 shorter events, 0.0 us)
Async XLA Ops:
  2.2 2.5 %collective-permute-start = (f32[384,128]{1,0:T(8,128)S(1)}, f32[384,128]{1,0:T(8,128)S(1)}, u32[]{:S(2)}, u32[]{:S(2)}) collective-permute-start(f32[384,128]{1,0:T(8,128)S(1)} %shard_map.85), channel_id=1, source_target_pairs={{0,1},{1,0},{2,3},{3,2},{4,5},{5,4},{6,7},{7,6},{8,9},{9,8},{10,11... | collective-permute-start | bytes 589832 | tf_op jit(solution)/shard_map/ppermute | solution.py:56
  4.8 35.0 %collective-permute-start.5 = (bf16[16,256,1024]{2,1,0:T(8,128)(2,1)}, bf16[16,256,1024]{2,1,0:T(8,128)(2,1)}, u32[]{:S(2)}, u32[]{:S(2)}) collective-permute-start(bf16[16,256,1024]{2,1,0:T(8,128)(2,1)} %bitcast.11), channel_id=1, source_target_pairs={{0,1},{1,0},{2,3},{3,2},{4,5},{5,4},{6,7},{7,6},{8,9},{9,8},{10,11... | collective-permute-start | bytes 25165832 | tf_op jit(solution)/shard_map/ppermute | solution.py:56
  6.8 4.3 %collective-permute-start.1 = (f32[192,128]{1,0:T(8,128)S(1)}, f32[192,128]{1,0:T(8,128)S(1)}, u32[]{:S(2)}, u32[]{:S(2)}) collective-permute-start(f32[192,128]{1,0:T(8,128)S(1)} %constant_dynamic-slice_fusion.1), channel_id=1, source_target_pairs={{0,2},{2,0},{1,3},{3,1},{4,6},{6,4},{5,7},{7,5},{8,10},{10,8},{9,1... | collective-permute-start | bytes 294920 | tf_op jit(solution)/shard_map/ppermute | solution.py:56
  12.1 24.5 %all-to-all-start = ((bf16[16,192,128]{2,1,0:T(8,128)(2,1)}), bf16[16,192,128]{2,1,0:T(8,128)(2,1)S(1)}, u32[]{:S(2)}, u32[]{:S(2)}) async-start(bf16[16,192,128]{2,1,0:T(8,128)(2,1)} %get-tuple-element.20), calls=%async_computation | async-start | bytes 1572864 | tf_op jit(solution)/shard_map/all_to_all | solution.py:52
  23.4 19.5 %collective-permute-start.6 = (bf16[384,1024]{1,0:T(8,128)(2,1)S(1)}, bf16[384,1024]{1,0:T(8,128)(2,1)S(1)}, u32[]{:S(2)}, u32[]{:S(2)}) collective-permute-start(bf16[384,1024]{1,0:T(8,128)(2,1)S(1)} %constant_dynamic-slice_fusion), channel_id=1, source_target_pairs={{0,1},{1,0},{2,3},{3,2},{4,5},{5,4},{6,7},{7,6},{8,9},{9,8},{10,11... | collective-permute-start | bytes 2359304 | tf_op jit(solution)/shard_map/ppermute | solution.py:56
  36.6 11.2 %collective-permute-start.2 = (bf16[16,192,128]{2,1,0:T(8,128)(2,1)S(1)}, bf16[16,192,128]{2,1,0:T(8,128)(2,1)}, u32[]{:S(2)}, u32[]{:S(2)}) collective-permute-start(bf16[16,192,128]{2,1,0:T(8,128)(2,1)S(1)} %all-to-all-done.block.firing.a), channel_id=1, source_target_pairs={{0,2},{1,7},{2,4},{3,1},{4,6},{5,3},{6,0},{7,5},{8,10},{9,15},{10,... | collective-permute-start | bytes 2359304 | tf_op jit(solution)/shard_map/ppermute | solution.py:48
  36.7 11.2 %collective-permute-start.3 = (bf16[16,192,128]{2,1,0:T(8,128)(2,1)S(1)}, bf16[16,192,128]{2,1,0:T(8,128)(2,1)S(1)}, u32[]{:S(2)}, u32[]{:S(2)}) collective-permute-start(bf16[16,192,128]{2,1,0:T(8,128)(2,1)S(1)} %all-to-all-done.block.firing.a), channel_id=1, source_target_pairs={{0,96},{1,25},{2,98},{3,27},{4,100},{5,29},{6,102},{7,31},{8,104},... | collective-permute-start | bytes 2359304 | tf_op jit(solution)/shard_map/ppermute | solution.py:48
  38.5 12.5 %collective-permute-start.4 = (bf16[16,192,128]{2,1,0:T(8,128)(2,1)S(1)}, bf16[16,192,128]{2,1,0:T(8,128)(2,1)S(1)}, u32[]{:S(2)}, u32[]{:S(2)}) collective-permute-start(bf16[16,192,128]{2,1,0:T(8,128)(2,1)S(1)} %all-to-all-done.block.firing.a), channel_id=1, source_target_pairs={{0,32},{1,9},{2,34},{3,11},{4,36},{5,13},{6,38},{7,15},{8,40},{9,1... | collective-permute-start | bytes 2359304 | tf_op jit(solution)/shard_map/ppermute | solution.py:48
  48.0 10.4 %copy-start.1 = (bf16[16,192,128]{2,1,0:T(8,128)(2,1)}, bf16[16,192,128]{2,1,0:T(8,128)(2,1)S(1)}, u32[]{:S(2)}) copy-start(bf16[16,192,128]{2,1,0:T(8,128)(2,1)S(1)} %collective-permute-done.3.a) | copy-start | bytes 2359300
  51.0 7.3 %copy-start.3 = (bf16[16,192,128]{2,1,0:T(8,128)(2,1)}, bf16[16,192,128]{2,1,0:T(8,128)(2,1)S(1)}, u32[]{:S(2)}) copy-start(bf16[16,192,128]{2,1,0:T(8,128)(2,1)S(1)} %collective-permute-done.4.b) | copy-start | bytes 2359300
  61.8 11.9 %collective-permute-start.7 = (bf16[16,208,128]{2,1,0:T(8,128)(2,1)S(1)}, bf16[16,208,128]{2,1,0:T(8,128)(2,1)S(1)}, u32[]{:S(2)}, u32[]{:S(2)}) collective-permute-start(bf16[16,208,128]{2,1,0:T(8,128)(2,1)S(1)} %get-tuple-element.28), channel_id=1, source_target_pairs={{32,0},{9,1},{34,2},{11,3},{36,4},{13,5},{38,6},{15,7},{40,8},{17,... | collective-permute-start | bytes 2555912 | tf_op jit(solution)/shard_map/ppermute | solution.py:48
  65.7 13.3 %collective-permute-start.8 = (bf16[16,208,128]{2,1,0:T(8,128)(2,1)S(1)}, bf16[16,208,128]{2,1,0:T(8,128)(2,1)S(1)}, u32[]{:S(2)}, u32[]{:S(2)}) collective-permute-start(bf16[16,208,128]{2,1,0:T(8,128)(2,1)S(1)} %get-tuple-element.29), channel_id=1, source_target_pairs={{2,0},{7,1},{4,2},{1,3},{6,4},{3,5},{0,6},{5,7},{10,8},{15,9},{12,... | collective-permute-start | bytes 2555912 | tf_op jit(solution)/shard_map/ppermute | solution.py:48
  66.0 13.1 %collective-permute-start.9 = (bf16[16,208,128]{2,1,0:T(8,128)(2,1)S(1)}, bf16[16,208,128]{2,1,0:T(8,128)(2,1)S(1)}, u32[]{:S(2)}, u32[]{:S(2)}) collective-permute-start(bf16[16,208,128]{2,1,0:T(8,128)(2,1)S(1)} %get-tuple-element.30), channel_id=1, source_target_pairs={{96,0},{25,1},{98,2},{27,3},{100,4},{29,5},{102,6},{31,7},{104,8},... | collective-permute-start | bytes 2555912 | tf_op jit(solution)/shard_map/ppermute | solution.py:48
  67.2 23.5 %collective-permute-start.16 = (bf16[16,192,128]{2,1,0:T(8,128)(2,1)S(1)}, bf16[16,192,128]{2,1,0:T(8,128)(2,1)}, u32[]{:S(2)}, u32[]{:S(2)}) collective-permute-start(bf16[16,192,128]{2,1,0:T(8,128)(2,1)S(1)} %all-to-all-done.block.firing.a), channel_id=1, source_target_pairs={{0,1},{1,0},{2,3},{3,2},{4,5},{5,4},{6,7},{7,6},{8,9},{9,8},{10,11... | collective-permute-start | bytes 2359304 | tf_op jit(solution)/shard_map/ppermute | solution.py:56
  72.2 18.5 %collective-permute-start.17 = (bf16[16,192,128]{2,1,0:T(8,128)(2,1)}, bf16[16,192,128]{2,1,0:T(8,128)(2,1)}, u32[]{:S(2)}, u32[]{:S(2)}) collective-permute-start(bf16[16,192,128]{2,1,0:T(8,128)(2,1)} %collective-permute-done.2.two.b), channel_id=1, source_target_pairs={{0,1},{1,0},{2,3},{3,2},{4,5},{5,4},{6,7},{7,6},{8,9},{9,8},{10,11... | collective-permute-start | bytes 2359304 | tf_op jit(solution)/shard_map/ppermute | solution.py:56
  73.7 16.9 %collective-permute-start.15 = (bf16[384,1024]{1,0:T(8,128)(2,1)S(1)}, bf16[384,1024]{1,0:T(8,128)(2,1)}, u32[]{:S(2)}, u32[]{:S(2)}) collective-permute-start(bf16[384,1024]{1,0:T(8,128)(2,1)S(1)} %get-tuple-element.24.signal_other), channel_id=1, source_target_pairs={{0,1},{1,0},{2,3},{3,2},{4,5},{5,4},{6,7},{7,6},{8,9},{9,8},{10,11... | collective-permute-start | bytes 2359304 | tf_op jit(solution)/shard_map/ppermute | solution.py:56
  80.5 17.6 %all-to-all-start.1 = ((bf16[16,208,128]{2,1,0:T(8,128)(2,1)}), bf16[16,208,128]{2,1,0:T(8,128)(2,1)S(1)}, u32[]{:S(2)}, u32[]{:S(2)}) async-start(bf16[16,208,128]{2,1,0:T(8,128)(2,1)} %shard_map.93), calls=%async_computation.1 | async-start | bytes 1703936 | tf_op jit(solution)/shard_map/all_to_all | solution.py:52
  85.2 19.7 %collective-permute-start.13 = (bf16[16,192,128]{2,1,0:T(8,128)(2,1)}, bf16[16,192,128]{2,1,0:T(8,128)(2,1)}, u32[]{:S(2)}, u32[]{:S(2)}) collective-permute-start(bf16[16,192,128]{2,1,0:T(8,128)(2,1)} %copy-done.1), channel_id=1, source_target_pairs={{0,1},{1,0},{2,3},{3,2},{4,5},{5,4},{6,7},{7,6},{8,9},{9,8},{10,11... | collective-permute-start | bytes 2359304 | tf_op jit(solution)/shard_map/ppermute | solution.py:56
  90.6 14.3 %collective-permute-start.14 = (bf16[16,192,128]{2,1,0:T(8,128)(2,1)}, bf16[16,192,128]{2,1,0:T(8,128)(2,1)}, u32[]{:S(2)}, u32[]{:S(2)}) collective-permute-start(bf16[16,192,128]{2,1,0:T(8,128)(2,1)} %copy-done.3), channel_id=1, source_target_pairs={{0,1},{1,0},{2,3},{3,2},{4,5},{5,4},{6,7},{7,6},{8,9},{9,8},{10,11... | collective-permute-start | bytes 2359304 | tf_op jit(solution)/shard_map/ppermute | solution.py:56
  98.2 16.0 %copy-start = (bf16[1,768,1024]{2,1,0:T(8,128)(2,1)S(1)}, bf16[1,768,1024]{2,1,0:T(8,128)(2,1)}, u32[]{:S(2)}) copy-start(bf16[1,768,1024]{2,1,0:T(8,128)(2,1)} %param.5) | copy-start | bytes 4718596
  98.2 16.0 %collective-permute-start.10 = (bf16[208,128]{1,0:T(8,128)(2,1)S(1)}, bf16[208,128]{1,0:T(8,128)(2,1)S(1)}, u32[]{:S(2)}, u32[]{:S(2)}) collective-permute-start(bf16[208,128]{1,0:T(8,128)(2,1)S(1)} %shard_map.94.own), channel_id=1, source_target_pairs={{0,2},{2,0},{1,3},{3,1},{4,6},{6,4},{5,7},{7,5},{8,10},{10,8},{9,1... | collective-permute-start | bytes 159752 | tf_op jit(solution)/shard_map/ppermute | solution.py:56
  101.4 12.8 %collective-permute-start.11 = (bf16[208,128]{1,0:T(8,128)(2,1)S(1)}, bf16[208,128]{1,0:T(8,128)(2,1)S(1)}, u32[]{:S(2)}, u32[]{:S(2)}) collective-permute-start(bf16[208,128]{1,0:T(8,128)(2,1)S(1)} %shard_map.94.own), channel_id=1, source_target_pairs={{0,1},{1,0},{2,3},{3,2},{4,5},{5,4},{6,7},{7,6},{8,9},{9,8},{10,11... | collective-permute-start | bytes 159752 | tf_op jit(solution)/shard_map/ppermute | solution.py:56
  104.6 9.6 %collective-permute-start.12 = (bf16[208,128]{1,0:T(8,128)(2,1)S(1)}, bf16[208,128]{1,0:T(8,128)(2,1)S(1)}, u32[]{:S(2)}, u32[]{:S(2)}) collective-permute-start(bf16[208,128]{1,0:T(8,128)(2,1)S(1)} %shard_map.94.own), channel_id=1, source_target_pairs={{0,3},{1,2},{2,1},{3,0},{4,7},{5,6},{6,5},{7,4},{8,11},{9,10},{10,... | collective-permute-start | bytes 159752 | tf_op jit(solution)/shard_map/ppermute | solution.py:576
  104.8 1.1 copy-start.2
  106.0 1.1 copy-start.4
